TPU v7x, 256 devices: a whole 4x4x8 slice. The times are simulated.
256 devices in a mesh: orb: 128 (over x_lo, z, y, core), grid: 2 (over x_hi).
Axes of the slice: x: 4 (x_hi: 2, x_lo: 2; x = x_hi * 2 + x_lo), y: 4, z: 8, core: 2. Of those that a mesh axis runs over, the one named last changes fastest.
Arguments:
- orbitals: bfloat16 [256, 11520], P('orb', 'grid'), may hold values from -1.5 to 1.5
- occupation: bfloat16 [256], P('orb'), may hold values from 0.29882812 to 1
Outputs:
- potentials: float32 [256, 11520], P('orb', 'grid')
- projectors: float32 [256, 11520], P('orb', 'grid')
All inputs are finite; a program needn't handle non-finite values.
Results may differ from a plain program's by a relative error of at most 0.0025.
Values may be sent and summed in bfloat16 or wider, within the bound.
A program may use at most 64 MiB of HBM per device.

v0:
```python
import math

import jax
import jax.numpy as jnp
from jax import lax
from jax.sharding import Mesh
from jax.sharding import PartitionSpec as P

NX = 20
NY = 24
NZ = 24
NPTS = 11520
ORB = ("orb_0", "orb_1", "orb_2", "orb_3")
ORB_GRID = ("orb_0", "orb_1", "orb_2", "orb_3", "grid")


def in_one_piece(arrays, axis, dim, along):
    columns = [a.reshape(*a.shape[:along], -1) for a in arrays]
    both = jnp.concatenate(columns, axis=along)
    whole, at, done = (lax.all_gather(both, axis, axis=dim, tiled=True), 0, [])
    for a, column in zip(arrays, columns):
        share = whole[..., at : at + column.shape[along]]
        done.append(share.reshape(*share.shape[:along], *a.shape[along:]))
        at += column.shape[along]
    return tuple(done)


def in_blocks(x, dim, count):
    dims = x.shape
    tiles = x.reshape(*dims[:dim], count, dims[dim] // count, *dims[dim + 1 :])
    return jnp.moveaxis(tiles, dim, 0)


def in_order(tiles, dim):
    dims = list(tiles.shape[1:])
    dims[dim] *= tiles.shape[0]
    return jnp.moveaxis(tiles, 0, dim).reshape(dims)


def moved_by_axis(tiles, axes, sequence):
    inside = tiles.shape[1:]
    whole = tiles.reshape(*(lax.axis_size(a) for a in axes), *inside)
    for k in sequence:
        whole = lax.all_to_all(whole, axes[k], k, k, tiled=True)
    return whole.reshape(-1, *inside)


def exchange_by_chip(x, groups, sequence, split_dim, concat_dim):
    count = lax.axis_size(groups[0]) * lax.axis_size(groups[1])
    tiles = in_blocks(x, split_dim, count)
    return in_order(moved_by_axis(tiles, groups, sequence), concat_dim)


def hartley_table(length):
    index = jnp.arange(length, dtype=jnp.int32)
    product = index[:, None] * index[None, :] % length
    angle = 2.0 * math.pi / length * product.astype(jnp.float32)
    return (jnp.cos(angle) + jnp.sin(angle)).astype(jnp.bfloat16)


def signed_square(length):
    index = jnp.arange(length, dtype=jnp.int32)
    signed = jnp.where(index <= length // 2, index, index - length).astype(jnp.float32)
    return (2.0 * math.pi * signed / length) ** 2


def coulomb_kernel(size_x, size_y, size_z):
    total = (
        signed_square(size_x)[:, None, None]
        + signed_square(size_y)[None, :, None]
        + signed_square(size_z)[None, None, :]
    )
    safe = jnp.where(total > 0, total, 1.0)
    return jnp.where(total > 0, 1.0 / safe, 0.0) / (size_x * size_y * size_z)


def solve_pairs(density, table_x, table_y, table_z, kernel):
    section = jnp.einsum(
        "ax,pxyz->payz", table_x, density, preferred_element_type=jnp.float32
    ).astype(jnp.bfloat16)
    section = jnp.einsum(
        "by,pxyz->pxbz", table_y, section, preferred_element_type=jnp.float32
    ).astype(jnp.bfloat16)
    spectrum = jnp.einsum("cz,pxyz->pxyc", table_z, section, preferred_element_type=jnp.float32)
    section = (spectrum * kernel).astype(jnp.bfloat16)
    section = jnp.einsum(
        "cz,pxyz->pxyc", table_z, section, preferred_element_type=jnp.float32
    ).astype(jnp.bfloat16)
    section = jnp.einsum(
        "by,pxyz->pxbz", table_y, section, preferred_element_type=jnp.float32
    ).astype(jnp.bfloat16)
    return jnp.einsum("ax,pxyz->payz", table_x, section, preferred_element_type=jnp.float32)


def pair_folder(targets, running, pieces):
    table_x = hartley_table(NX)
    table_y = hartley_table(NY)
    table_z = hartley_table(NZ)
    kernel = coulomb_kernel(NX, NY, NZ)
    target_rows = targets.astype(jnp.float32)
    target_count = targets.shape[0]
    block, block_weight = pieces
    rows = block.shape[0]
    group = math.gcd(rows, 64)
    blocks = block.reshape(rows // group, group, NPTS)
    weights = block_weight.astype(jnp.float32).reshape(rows // group, group)

    def accumulate(totals, inputs):
        sources, source_weight = inputs
        source_rows = sources.astype(jnp.float32)
        density = (target_rows[:, None, :] * source_rows[None, :, :]).astype(jnp.bfloat16)
        density = density.reshape(target_count * group, NX, NY, NZ)
        potential = solve_pairs(density, table_x, table_y, table_z, kernel).reshape(
            target_count, group, NPTS
        )
        weighted = source_weight[None, :, None] * potential * source_rows[None, :, :]
        return (totals - jnp.sum(weighted, axis=1), None)

    result, unused = lax.scan(accumulate, running, (blocks, weights))
    return result


def on_device(orbitals, occupation):
    own_count = orbitals.shape[0]
    per_device = own_count // lax.axis_size("grid")
    empty = jnp.zeros((per_device, NPTS), jnp.float32)
    whole = lax.all_gather(orbitals, "grid", axis=1, tiled=True)
    targets = lax.dynamic_slice_in_dim(whole, lax.axis_index("grid") * per_device, per_device, 0)
    totals = pair_folder(targets, empty, in_one_piece((whole, occupation), ORB, 0, 1))
    potentials = lax.all_to_all(totals, "grid", split_axis=1, concat_axis=0, tiled=True)
    source_points, potential_points = (
        exchange_by_chip(
            orbitals.astype(jnp.float32), (("orb_0", "orb_1", "orb_2"), "orb_3"), (0, 1), 1, 0
        ),
        exchange_by_chip(potentials, (("orb_0", "orb_1", "orb_2"), "orb_3"), (0, 1), 1, 0),
    )
    partial_gram = (
        lax.dot_general(
            source_points,
            potential_points,
            (((1,), (1,)), ((), ())),
            precision=lax.Precision.HIGHEST,
        )
        / NPTS
    )
    gram = lax.psum(partial_gram, ORB_GRID)
    factor = jnp.linalg.cholesky(-gram)
    identity = jnp.eye(gram.shape[0], dtype=jnp.float32)
    inverse = lax.linalg.triangular_solve(factor, identity, left_side=True, lower=True)
    projector_points = jnp.dot(inverse, potential_points, precision=lax.Precision.HIGHEST)
    projectors = exchange_by_chip(
        projector_points, (("orb_0", "orb_1", "orb_2"), "orb_3"), (1, 0), 0, 1
    )
    return (potentials, projectors)


def solution(mesh):
    torus = Mesh(
        mesh.devices.reshape(2, 8, 4, 2, mesh.shape["grid"]),
        ("orb_0", "orb_1", "orb_2", "orb_3", "grid"),
    )
    placed = (P(ORB, "grid"), P(ORB))
    return jax.shard_map(
        on_device,
        mesh=torus,
        in_specs=placed,
        out_specs=(P(ORB, "grid"), P(ORB, "grid")),
        check_vma=False,
    )
```

profile of v0, /device:TPU:1, one launch (start us, length us, event | category | flops | bytes accessed | tf_op | source)
XLA Modules:
  0.0 773.7 jit_solution(7123645423306138331)
XLA Ops:
  7.2 5.7 all_gather.6
  16.2 12.9 %all-to-all-start.3 = ((f32[64,1,180]{2,1,0:T(1,128)}), f32[64,1,180]{2,1,0:T(1,128)S(1)}, u32[]{:S(2)}, u32[]{:S(2)}) async-start(f32[64,1,180]{2,1,0:T(1,128)} %reshape.240), calls=%async_computation.3 | async-start | bytes 131072 | tf_op jit(solution)/shard_map/all_to_all | solution.py:44
  29.3 206.2 %all-gather.3.cloned.1.call-done = bf16[128,2,11521]{2,1,0:T(2,128)(2,1)} async-done(((bf16[1,2,11521]{2,1,0:T(2,128)(2,1)}), bf16[128,2,11521]{2,1,0:T(2,128)(2,1)}) %all-gather.3.cloned.1.call-update) | async-done | bytes 5898768 | tf_op jit(solution)/shard_map/all_gather | solution.py:20
  235.5 12.9 %reshape.227 = bf16[256,11521]{1,0:T(8,128)(2,1)} reshape(bf16[128,2,11521]{2,1,0:T(2,128)(2,1)} %all-gather.3.cloned.1.call-done) | data formatting | bytes 11797504
  248.4 5.6 slice.63
  255.0 133.5 %while.15 = (s32[]{:T(128)}, f32[1,11520]{1,0:T(1,128)}, f32[4,64]{1,0:T(4,128)S(1)}, f32[1,11520]{1,0:T(1,128)S(1)}, bf16[4,64,11520]{2,1,0:T(8,128)(2,1)}, /*i...) while((s32[]{:T(128)}, f32[1,11520]{1,0:T(1,128)}, ...), condition=%wide.region_2.3_spmd.clone.clone, body=%wide.region_0.2_spmd.clone.clone.sunk | while | flops 210239584 | bytes 35807064 | solution.py:119
  255.2 2.6 constant_dynamic-slice_fusion.5
  257.8 3.0 copy.123
  261.0 4.9 fusion.150
  267.9 5.2 convert_bitcast_fusion.7
  273.2 4.7 fusion.151
  278.0 2.8 convert_bitcast_fusion.8
  280.8 3.5 fusion.152
  287.9 2.6 constant_dynamic-slice_fusion.5
  290.5 3.0 copy.123
  293.7 4.9 fusion.150
  300.6 5.2 convert_bitcast_fusion.7
  305.9 4.7 fusion.151
  310.7 2.8 convert_bitcast_fusion.8
  313.5 3.5 fusion.152
  321.4 2.6 constant_dynamic-slice_fusion.5
  324.0 3.0 copy.123
  327.1 4.9 fusion.150
  334.1 5.2 convert_bitcast_fusion.7
  339.4 4.7 fusion.151
  344.1 2.8 convert_bitcast_fusion.8
  346.9 3.5 fusion.152
  354.8 2.6 constant_dynamic-slice_fusion.5
  357.5 3.0 copy.123
  360.6 4.9 fusion.150
  367.6 5.2 convert_bitcast_fusion.7
  372.9 4.7 fusion.151
  377.6 2.8 convert_bitcast_fusion.8
  380.4 3.5 fusion.152
  388.5 4.3 all-to-all-start
  397.2 5.8 all-to-all-start.4
  404.3 7.3 all-to-all-start.1
  412.7 8.5 %all-to-all-done.1 = f32[64,1,180]{2,1,0:T(1,128)S(1)} async-done(((f32[64,1,180]{2,1,0:T(1,128)}), f32[64,1,180]{2,1,0:T(1,128)S(1)}, u32[]{:S(2)}, u32[]{:S(2)}) %all-to-all-start.1) | async-done | bytes 46112 | tf_op jit(solution)/shard_map/all_to_all | solution.py:44
  422.5 5.0 all_to_all.46
  429.7 245.2 %all-reduce.3.cloned.1.call-done = f32[256,256]{0,1:T(8,128)} async-done(((f32[256,256]{0,1:T(8,128)}), f32[256,256]{0,1:T(8,128)}) %all-reduce.3.cloned.1.call-update) | async-done | bytes 262160 | tf_op jit(solution)/shard_map/psum | solution.py:146
  677.1 11.7 %cholesky.50 = f32[128,128]{1,0:T(8,128)S(1)} custom-call(f32[128,128]{1,0:T(8,128)S(1)} %cholesky.118), custom_call_target="Cholesky" | custom-call | tf_op jit(solution)/shard_map/jit(cholesky)/cholesky | solution.py:147
  688.8 9.8 %custom-call.14 = f32[1,128,128]{1,2,0:T(8,128)S(1)} custom-call(f32[1,128,128]{2,1,0:T(8,128)S(1)} %get-tuple-element.199), custom_call_target="InvertDiagBlocksLowerTriangular" | custom-call | tf_op jit(solution)/shard_map/jit(cholesky)/cholesky | solution.py:147
  699.2 11.7 %cholesky.105 = f32[128,128]{1,0:T(8,128)S(1)} custom-call(f32[128,128]{1,0:T(8,128)S(1)} %convolution_subtract_fusion.1), custom_call_target="Cholesky" | custom-call | tf_op jit(solution)/shard_map/jit(cholesky)/cholesky | solution.py:147
  713.0 4.2 while.14
  717.2 19.7 %custom-call.15 = f32[2,128,128]{1,2,0:T(8,128)S(1)} custom-call(f32[2,128,128]{2,1,0:T(8,128)S(1)} %get-tuple-element.86), custom_call_target="InvertDiagBlocksLowerTriangular" | custom-call | tf_op jit(solution)/shard_map/triangular_solve | solution.py:149
  738.6 5.8 all_to_all.47
  746.3 8.5 %all-to-all-start.6 = ((f32[64,1,180]{2,1,0:T(1,128)}), f32[64,1,180]{2,1,0:T(1,128)S(1)}, u32[]{:S(2)}, u32[]{:S(2)}) async-start(f32[64,1,180]{2,1,0:T(1,128)} %reshape.246), calls=%async_computation.6 | async-start | bytes 131072 | tf_op jit(solution)/shard_map/all_to_all | solution.py:44
  755.4 9.0 %all-to-all-done.6 = f32[64,1,180]{2,1,0:T(1,128)S(1)} async-done(((f32[64,1,180]{2,1,0:T(1,128)}), f32[64,1,180]{2,1,0:T(1,128)S(1)}, u32[]{:S(2)}, u32[]{:S(2)}) %all-to-all-start.6) | async-done | bytes 46112 | tf_op jit(solution)/shard_map/all_to_all | solution.py:44
  (105 shorter events, 54.4 us)
Async XLA Ops:
  7.2 228.3 %all-gather.3.cloned.1.call-start = ((), (), s32[]{:S(2)}) async-start(), calls=%async_computation.8 | async-start | bytes 6010368 | tf_op jit(solution)/shard_map/all_gather | solution.py:20
  16.2 372.3 %all-to-all-start.3 = ((f32[64,1,180]{2,1,0:T(1,128)}), f32[64,1,180]{2,1,0:T(1,128)S(1)}, u32[]{:S(2)}, u32[]{:S(2)}) async-start(f32[64,1,180]{2,1,0:T(1,128)} %reshape.240), calls=%async_computation.3 | async-start | bytes 131072 | tf_op jit(solution)/shard_map/all_to_all | solution.py:44
  388.5 8.7 %all-to-all-start = ((f32[1,2,5760]{2,0,1:T(1,128)}), f32[1,2,5760]{2,0,1:T(1,128)S(1)}, u32[]{:S(2)}, u32[]{:S(2)}) async-start(f32[1,2,5760]{2,0,1:T(1,128)} %bitcast.3), calls=%async_computation | async-start | bytes 92160 | tf_op jit(solution)/shard_map/all_to_all | solution.py:130
  397.2 7.1 all-to-all-start.4
  404.3 16.9 %all-to-all-start.1 = ((f32[64,1,180]{2,1,0:T(1,128)}), f32[64,1,180]{2,1,0:T(1,128)S(1)}, u32[]{:S(2)}, u32[]{:S(2)}) async-start(f32[64,1,180]{2,1,0:T(1,128)} %reshape.236), calls=%async_computation.1 | async-start | bytes 131072 | tf_op jit(solution)/shard_map/all_to_all | solution.py:44
  411.6 263.4 %all-reduce.3.cloned.1.call-start = ((), (), s32[]{:S(2)}) async-start(), calls=%async_computation.7 | async-start | bytes 524288 | tf_op jit(solution)/shard_map/psum | solution.py:146
  746.3 18.2 %all-to-all-start.6 = ((f32[64,1,180]{2,1,0:T(1,128)}), f32[64,1,180]{2,1,0:T(1,128)S(1)}, u32[]{:S(2)}, u32[]{:S(2)}) async-start(f32[64,1,180]{2,1,0:T(1,128)} %reshape.246), calls=%async_computation.6 | async-start | bytes 131072 | tf_op jit(solution)/shard_map/all_to_all | solution.py:44
Sparse Core Ops, SparseCore 0:
  14.5 220.9 all-gather.2
  429.8 245.1 all-reduce.2
where the time goes:
time: 784 us; the launch traced here: 774 us
  waiting for transfers between devices  471 us (60%)
  other arithmetic  95.2 us (12%)
  matrix products  75.9 us (10%)
  local copies, waits for them, and re-layouts  59.3 us (8%)
  starting transfers between devices  38.9 us (5%)
  blocking collectives  16.4 us (2%)
  between operations  16.1 us (2%)
    psum x1, waiting for transfers between devices, on_device(): gram = lax.psum(partial_gram, ORB_GRID)  245 us
    all_gather x1, waiting for transfers between devices, in_one_piece(): whole, at, done = (lax.all_gather(both, axis, axis=dim, tiled=True), 0, [])  206 us
    all_to_all x4, starting transfers between devices, moved_by_axis(): whole = lax.all_to_all(whole, axes[k], k, k, tiled=True)  34.5 us
    another operation x6, other arithmetic, on_device(): factor = jnp.linalg.cholesky(-gram)  34 us
    dot_general x8, matrix products, solve_pairs(): jnp.einsum('by,pxyz->pxbz', table_y, section, preferred_element_type=jnp....  31.9 us
    dynamic_slice x12, local copies, waits for them, and re-layouts, pair_folder(): result, unused = lax.scan(accumulate, running, (blocks, weights))  22.6 us
    another operation x4, other arithmetic, on_device(): lax.linalg.triangular_solve(factor, identity, left_side=True, lower=True)  19.7 us
    convert_element_type x4, other arithmetic, accumulate(): (target_rows[:, None, :] * source_rows[None, :, :]).astype(jnp.bfloat16)  19.4 us
  transfers between devices with their start and end apart: 7, of which 5 were waited for; matrix products, arithmetic and copies ran while one was open for 21% of the time, Pallas kernels for 0%

commit v1 on v0

v1 whole, which is shorter than its diff:
```python
import functools
import math

import jax
import jax.numpy as jnp
import numpy as np
from jax import lax
from jax.experimental import pallas as pl
from jax.experimental.pallas import tpu as pltpu
from jax.sharding import Mesh
from jax.sharding import PartitionSpec as P

NX = 20
NY = 24
NZ = 24
NORB = 256
NPTS = 11520
HALF = NPTS // 2
MODES = 512
ROWS = 384
AXES = ("xl", "z", "y", "c", "h")
ORB = ("xl", "z", "y", "c")
MESH = pl.DeviceIdType.MESH
F32 = jnp.float32
BF16 = jnp.bfloat16


def rounded(a):
    return np.asarray(a, np.float32).astype(jnp.bfloat16).astype(np.float32)


def hartley_table(length):
    index = np.arange(length)
    angle = 2.0 * math.pi / length * (index[:, None] * index[None, :] % length)
    return rounded(np.cos(angle) + np.sin(angle))


def signed_square(length):
    index = np.arange(length)
    signed = np.where(index <= length // 2, index, index - length)
    return (2.0 * math.pi * signed / length) ** 2


def coulomb_kernel():
    total = (
        signed_square(NX)[:, None, None]
        + signed_square(NY)[None, :, None]
        + signed_square(NZ)[None, None, :]
    )
    return np.where(total > 0, 1.0 / np.where(total > 0, total, 1.0), 0.0) / NPTS


def two_parts(a):
    high = rounded(a)
    return high, rounded(a - high)


def tables():
    cx, cy, cz = hartley_table(NX), hartley_table(NY), hartley_table(NZ)
    kernel = coulomb_kernel()
    ac = NX * NZ
    tx = np.zeros((128, MODES), np.float32)
    tx[:NX, :ac] = np.repeat(cx, NZ, axis=1)
    tz = np.zeros((128, MODES), np.float32)
    tz[:NZ, :ac] = np.tile(cz, (1, NX))
    ty = np.zeros((128, 128), np.float32)
    tk = np.zeros((128, MODES), np.float32)
    k_high, k_low = two_parts(kernel.transpose(1, 0, 2).reshape(NY, ac))
    for at, part in ((0, k_high), (32, k_high), (64, k_low)):
        ty[:NY, at : at + NY] = cy
        tk[at : at + NY, :ac] = part
    phi = np.einsum("ax,cz->acxz", cx, cz).reshape(ac, NX, NZ)
    right = np.zeros((MODES, 2, 256), np.float32)
    for h in range(2):
        right[:ac, h, :240] = phi[:, 10 * h : 10 * h + 10].reshape(ac, 240)
    r_high, r_low = two_parts(right.reshape(MODES, 512))
    bf = lambda a: jnp.asarray(a, BF16)
    return bf(tx), bf(tz), bf(ty), bf(tk), bf(r_high), bf(r_low), jnp.asarray(ty[:32], F32)


def permutations():
    true = np.arange(NORB).reshape(2, 8, 8, 2)
    order_a = true.transpose(0, 2, 1, 3).reshape(-1)
    order_b = true.transpose(1, 0, 2, 3).reshape(-1)
    eye = np.eye(NORB, dtype=np.float32)
    return tuple(jnp.asarray(eye[:, o], BF16) for o in (order_a, order_b))


def split2(a):
    high = a.astype(BF16)
    return high, (a - high.astype(F32)).astype(BF16)


def dot(a, b, dims=(1, 0)):
    return lax.dot_general(
        a, b, (((dims[0],), (dims[1],)), ((), ())), preferred_element_type=F32
    )


def me():
    return tuple(lax.axis_index(a) for a in AXES)


def of_plane(pid, z):
    return ((pid // 8) % 2, z, (pid // 2) % 4, pid % 2, pid // 16)


def copy(src, dst, send_sem, recv_sem, device):
    return pltpu.make_async_remote_copy(
        src_ref=src, dst_ref=dst, send_sem=send_sem, recv_sem=recv_sem,
        device_id=device, device_id_type=MESH,
    )


def rows(start, size):
    return pl.ds(pl.multiple_of(start, size), size)


def each(count, body):
    lax.fori_loop(0, count, lambda i, carry: (body(i), carry)[1], 0)


def gather_kernel(s1, s2, o1, o2, r1, r2, za_s, za_r, pa_s, pa_r, pg_s, pg_r, zg_s, zg_r):
    xl, z, y, c, h = me()
    p = xl * 8 + y * 2 + c
    pid = h * 16 + p

    z_dev = lambda t: (xl, t, y, c, h)
    half_dev = lambda t: of_plane(h * 16 + t, z)
    plane_dev = lambda t: of_plane(t, z)
    z_peer = lambda d: (z + d) % 8
    p_peer = lambda d: (p + d) % 16
    pid_peer = lambda d: (pid + d) % 32

    barrier = pltpu.get_barrier_semaphore()

    def hello(dev):
        pl.semaphore_signal(barrier, inc=1, device_id=dev, device_id_type=MESH)

    each(7, lambda d: hello(z_dev(z_peer(d + 1))))
    each(31, lambda d: hello(plane_dev(pid_peer(d + 1))))
    pl.semaphore_wait(barrier, 38)

    def z_send(t):
        return copy(s1.at[t], r1.at[rows(z * 16, 16)], za_s.at[t], za_r.at[z], z_dev(t))

    def z_recv(t):
        return copy(s1.at[t], r1.at[rows(t * 16, 16)], za_s.at[t], za_r.at[t], z_dev(t))

    def p_send(t):
        return copy(s2.at[t], r2.at[rows(p * 8, 8)], pa_s.at[t], pa_r.at[p], half_dev(t))

    def p_recv(t):
        return copy(s2.at[t], r2.at[rows(t * 8, 8)], pa_s.at[t], pa_r.at[t], half_dev(t))

    each(7, lambda d: z_send(z_peer(d + 1)).start())
    each(15, lambda d: p_send(p_peer(d + 1)).start())
    r1[rows(z * 16, 16)] = s1[z]
    r2[rows(p * 8, 8)] = s2[p]
    each(7, lambda d: z_recv(z_peer(d + 1)).wait_recv())
    for t in range(3):
        o1[h, rows(p * 16, 16), t * 256 : (t + 1) * 256] = jnp.concatenate(
            [r1[pl.ds(2 * t + k, 16, stride=8), :] for k in range(2)], axis=1
        ).astype(BF16)

    def g_send(t):
        mine = o1.at[h, rows(p * 16, 16)]
        return copy(mine, mine, pg_s.at[t], pg_r.at[pid], plane_dev(t))

    def g_recv(t):
        theirs = o1.at[t // 16, rows((t % 16) * 16, 16)]
        return copy(theirs, theirs, pg_s.at[t], pg_r.at[t], plane_dev(t))

    each(31, lambda d: g_send(pid_peer(d + 1)).start())
    each(15, lambda d: p_recv(p_peer(d + 1)).wait_recv())
    for k in range(4):
        o2[z, :, k * 128 : (k + 1) * 128] = r2[pl.ds(k, 32, stride=4), :].astype(BF16)

    def zg_send(t):
        return copy(o2.at[z], o2.at[z], zg_s.at[t], zg_r.at[z], z_dev(t))

    def zg_recv(t):
        return copy(o2.at[t], o2.at[t], zg_s.at[t], zg_r.at[t], z_dev(t))

    each(7, lambda d: zg_send(z_peer(d + 1)).start())
    each(7, lambda d: zg_recv(z_peer(d + 1)).wait_recv())
    each(31, lambda d: g_recv(pid_peer(d + 1)).wait_recv())
    each(7, lambda d: z_send(z_peer(d + 1)).wait_send())
    each(15, lambda d: p_send(p_peer(d + 1)).wait_send())
    each(31, lambda d: g_send(pid_peer(d + 1)).wait_send())
    each(7, lambda d: zg_send(z_peer(d + 1)).wait_send())


def potential_kernel(where, o1, o2, perm_a, perm_b, tx, tz, ty, tk, rh, rl, cy, v_out, g_out, green):
    p, h, z = where[0], where[1], where[2]
    row = lax.broadcasted_iota(jnp.int32, (ROWS, 128), 0)
    lane = lax.broadcasted_iota(jnp.int32, (ROWS, 128), 1)

    def over(a, n):
        return ((a.astype(F32) + 0.5) * (1.0 / n)).astype(jnp.int32)

    zz = over(row, 48)
    s = row - zz * 48
    cell = h * HALF + s * 128 + zz * 16 + p
    x = over(cell, NY * NZ)
    yz = cell - x * (NY * NZ)
    y = over(yz, NZ)
    z_cell = yz - y * NZ
    x = jnp.where(s < 45, x, 127)
    hot = lambda a: jnp.where(a == lane, 1.0, 0.0).astype(BF16)
    left = dot(hot(x), tx[...]) * dot(hot(z_cell), tz[...])
    y_rows = dot(hot(y), ty[...])
    middle = (lane >= 32) & (lane < 64)
    for t in range(3):
        q = y_rows * cy[pl.ds(z * 3 + t, 1), :]
        q_high, q_low = split2(q)
        mix = jnp.where(middle, q_low.astype(F32), q_high.astype(F32)).astype(BF16)
        l_high, l_low = split2(left * dot(mix, tk[...]))
        g = dot(l_high, rh[...]) + dot(l_low, rh[...]) + dot(l_high, rl[...])
        for hh in range(2):
            green[hh, :, t * 256 : (t + 1) * 256] = g[:, hh * 256 : (hh + 1) * 256]

    o_rows = dot(perm_b[...], o2[...])
    occ = o_rows[:, ROWS:]
    o_rows = o_rows[:, :ROWS]
    w = jnp.concatenate([o_rows[:, k * 128 : (k + 1) * 128] * occ for k in range(3)], axis=1)
    w = w.astype(BF16).T
    v = jnp.zeros((ROWS, NORB), F32)
    for hh in range(2):
        orb = dot(perm_a[...], o1[hh]).astype(BF16)
        m_high, m_low = split2(green[hh] * dot(w, orb))
        v = v + dot(m_high, orb, (1, 1)) + dot(m_low, orb, (1, 1))
    v_out[...] = v
    v_high, v_low = split2(v)
    o_b = o_rows.astype(BF16)
    g_out[...] = (dot(o_b, v_high) + dot(o_b, v_low)) * (1.0 / NPTS)


def reduce_kernel(gp, v, gram, vs, rg, rv, s8, rz, ga_s, ga_r, va_s, va_r, gz_s, gz_r, gg_s, gg_r):
    xl, z, y, c, h = me()
    pid = h * 16 + xl * 8 + y * 2 + c
    z_dev = lambda t: (xl, t, y, c, h)
    plane_dev = lambda t: of_plane(t, z)
    z_peer = lambda d: (z + d) % 8
    pid_peer = lambda d: (pid + d) % 32
    barrier = pltpu.get_barrier_semaphore()

    def hello(dev):
        pl.semaphore_signal(barrier, inc=1, device_id=dev, device_id_type=MESH)

    each(7, lambda d: hello(z_dev(z_peer(d + 1))))
    each(31, lambda d: hello(plane_dev(pid_peer(d + 1))))
    pl.semaphore_wait(barrier, 38)

    def a_send(t):
        return copy(gp.at[rows(t * 8, 8)], rg.at[pid], ga_s.at[t], ga_r.at[pid], plane_dev(t))

    def a_recv(t):
        return copy(gp.at[rows(t * 8, 8)], rg.at[t], ga_s.at[t], ga_r.at[t], plane_dev(t))

    def v_send(t):
        return copy(v.at[rows(t * 48, 48)], rv.at[z], va_s.at[t], va_r.at[z], z_dev(t))

    def v_recv(t):
        return copy(v.at[rows(t * 48, 48)], rv.at[t], va_s.at[t], va_r.at[t], z_dev(t))

    each(31, lambda d: a_send(pid_peer(d + 1)).start())
    each(7, lambda d: v_send(z_peer(d + 1)).start())
    rg[pid] = gp[rows(pid * 8, 8)]
    rv[z] = v[rows(z * 48, 48)]
    each(31, lambda d: a_recv(pid_peer(d + 1)).wait_recv())
    s8[...] = jnp.sum(rg[...], axis=0)
    rz[z] = s8[...]

    def z_send(t):
        return copy(s8, rz.at[z], gz_s.at[t], gz_r.at[z], z_dev(t))

    def z_recv(t):
        return copy(s8, rz.at[t], gz_s.at[t], gz_r.at[t], z_dev(t))

    each(7, lambda d: z_send(z_peer(d + 1)).start())
    each(7, lambda d: z_recv(z_peer(d + 1)).wait_recv())
    gram[rows(pid * 8, 8)] = jnp.sum(rz[...], axis=0)

    def g_send(t):
        mine = gram.at[rows(pid * 8, 8)]
        return copy(mine, mine, gg_s.at[t], gg_r.at[pid], plane_dev(t))

    def g_recv(t):
        theirs = gram.at[rows(t * 8, 8)]
        return copy(theirs, theirs, gg_s.at[t], gg_r.at[t], plane_dev(t))

    each(31, lambda d: g_send(pid_peer(d + 1)).start())
    each(7, lambda d: v_recv(z_peer(d + 1)).wait_recv())
    vs[...] = -jnp.sum(rv[...], axis=0)
    each(31, lambda d: g_recv(pid_peer(d + 1)).wait_recv())
    each(31, lambda d: a_send(pid_peer(d + 1)).wait_send())
    each(7, lambda d: v_send(z_peer(d + 1)).wait_send())
    each(7, lambda d: z_send(z_peer(d + 1)).wait_send())
    each(31, lambda d: g_send(pid_peer(d + 1)).wait_send())


def factor_kernel(gram, vs, dv, dq, work, left):
    a = gram[...]
    work[...] = (a + a.T) * 0.5
    sub = lax.broadcasted_iota(jnp.int32, (8, 128), 0)
    lane = lax.broadcasted_iota(jnp.int32, (8, 128), 1)
    wide = lambda col: jnp.broadcast_to(col, (8, 128))
    for k in range(8):
        base = 32 * k
        tile, off = base // 128, base % 128
        wk = [
            [work[base + 8 * g : base + 8 * g + 8, 128 * t : 128 * t + 128] for t in range(2)]
            for g in range(4)
        ]
        col = [
            [wide(wk[g][tile][:, off + j : off + j + 1]) if g >= j // 8 else None for g in range(4)]
            for j in range(32)
        ]
        inside = (lane >= off) & (lane < off + 32)
        for g in range(4):
            unit = jnp.where(lane - off == sub + 8 * g, 1.0, 0.0)
            wk[g][tile] = jnp.where(inside, unit, wk[g][tile])
        pivots = [jnp.ones((8, 128), F32) for _ in range(4)]
        for j in range(32):
            gj, sj = j // 8, j % 8
            d = wide(col[j][gj][sj : sj + 1, :])
            pivots[gj] = jnp.where(sub == sj, d, pivots[gj])
            r = 1.0 / d
            m = [None] * 4
            for g in range(gj, 4):
                m[g] = col[j][g] * r
                if g == gj:
                    m[g] = jnp.where(sub > sj, m[g], 0.0)
            for i in range(j + 1, 32):
                f = wide(col[j][i // 8][i % 8 : i % 8 + 1, :])
                for g in range(i // 8, 4):
                    col[i][g] = col[i][g] - m[g] * f
            for t in range(2):
                line = wide(wk[gj][t][sj : sj + 1, :])
                for g in range(gj, 4):
                    wk[g][t] = wk[g][t] - m[g] * line
        for g in range(4):
            scale = lax.rsqrt(pivots[g])
            for t in range(2):
                wk[g][t] = wk[g][t] * scale
        u = jnp.concatenate([jnp.concatenate(wk[g], axis=1) for g in range(4)], axis=0)
        lanes = lax.broadcasted_iota(jnp.int32, (32, 256), 1)
        work[base : base + 32, :] = jnp.where(lanes < base + 32, u, 0.0)
        if k < 7:
            u_high, u_low = split2(u)
            one = jnp.concatenate([u_high, u_low, u_high], axis=0)
            two = jnp.concatenate([u_high, u_high, u_low], axis=0)
            edge = base + 32
            start = edge // 128 * 128
            change = dot(one[:, start:].T, two)[edge - start :]
            rest = work[edge:, :]
            lanes = lax.broadcasted_iota(jnp.int32, rest.shape, 1)
            rest = jnp.where((lanes >= base) & (lanes < edge), 0.0, rest)
            work[edge:, :] = rest - change

    slab = vs[...]
    gap = jnp.zeros((16, NORB), F32)
    both = jnp.concatenate([slab, gap, slab, gap], axis=0)
    lane8 = lane < 64

    def deal(out):
        for p in range(16):
            base = (p // 8) * 128 + (p % 8) * 2
            even = left[pl.ds(base, 8, stride=16), :]
            odd = left[pl.ds(base + 1, 8, stride=16), :]
            out[p] = jnp.where(lane8, even, odd)

    left[...] = both.T
    deal(dv)
    l_high, l_low = split2(work[...])
    b_high, b_low = split2(both)
    left[...] = (
        dot(l_high, b_high, (1, 1)) + dot(l_low, b_high, (1, 1)) + dot(l_high, b_low, (1, 1))
    )
    deal(dq)


def return_kernel(dv, dq, ov, oq, rp, sz, rz, pa_s, pa_r, za_s, za_r):
    xl, z, y, c, h = me()
    p = xl * 8 + y * 2 + c
    z_dev = lambda t: (xl, t, y, c, h)
    half_dev = lambda t: of_plane(h * 16 + t, z)
    z_peer = lambda d: (z + d) % 8
    p_peer = lambda d: (p + d) % 16
    barrier = pltpu.get_barrier_semaphore()

    def hello(dev):
        pl.semaphore_signal(barrier, inc=1, device_id=dev, device_id_type=MESH)

    each(7, lambda d: hello(z_dev(z_peer(d + 1))))
    each(15, lambda d: hello(half_dev(p_peer(d + 1))))
    pl.semaphore_wait(barrier, 22)

    def p_send(n, t):
        src = (dv, dq)[n]
        return copy(src.at[t], rp.at[n, rows(p * 8, 8)], pa_s.at[n, t], pa_r.at[n, p], half_dev(t))

    def p_recv(n, t):
        src = (dv, dq)[n]
        return copy(src.at[t], rp.at[n, rows(t * 8, 8)], pa_s.at[n, t], pa_r.at[n, t], half_dev(t))

    def z_send(n, t):
        return copy(sz.at[n, t], rz.at[n, rows(z * 16, 16)], za_s.at[n, t], za_r.at[n, z], z_dev(t))

    def z_recv(n, t):
        return copy(sz.at[n, t], rz.at[n, rows(t * 16, 16)], za_s.at[n, t], za_r.at[n, t], z_dev(t))

    for n in range(2):
        each(15, lambda d: p_send(n, p_peer(d + 1)).start())
        rp[n, rows(p * 8, 8)] = (dv, dq)[n][p]
    for n in range(2):
        each(15, lambda d: p_recv(n, p_peer(d + 1)).wait_recv())
        for t in range(8):
            sz[n, t] = rp[n, pl.ds(t, 16, stride=8), :]
        each(7, lambda d: z_send(n, z_peer(d + 1)).start())
        rz[n, rows(z * 16, 16)] = sz[n, z]
    for n in range(2):
        each(7, lambda d: z_recv(n, z_peer(d + 1)).wait_recv())
        out = (ov, oq)[n]
        turned = rz[n].T
        for o in range(2):
            out[o] = turned[64 * o : 64 * o + 48]
    for n in range(2):
        each(15, lambda d: p_send(n, p_peer(d + 1)).wait_send())
        each(7, lambda d: z_send(n, z_peer(d + 1)).wait_send())


VM = pl.BlockSpec(memory_space=pltpu.VMEM)
SM = pl.BlockSpec(memory_space=pltpu.SMEM)
DMA = pltpu.SemaphoreType.DMA


def call(kernel, args, outs, scratch, number=None, name=None, specs=None):
    params = dict(vmem_limit_bytes=60 * 1024 * 1024)
    if number is not None:
        params.update(collective_id=number, has_side_effects=True)
    return pl.pallas_call(
        kernel,
        out_shape=[jax.ShapeDtypeStruct(s, d) for s, d in outs],
        in_specs=specs or [VM] * len(args),
        out_specs=[VM] * len(outs),
        scratch_shapes=scratch,
        compiler_params=pltpu.CompilerParams(**params),
        name=name,
    )(*args)


def on_device(orbitals, occupation):
    xl, z, y, c, h = me()
    own = orbitals.astype(F32)
    s1 = own.reshape(2, 10, 8, 3, NZ).transpose(2, 0, 3, 1, 4).reshape(8, 2, 3, 240)
    s1 = jnp.pad(s1, ((0, 0), (0, 0), (0, 1), (0, 16))).reshape(8, 16, 128)
    s2 = own.reshape(2, 45, 8, 16).transpose(3, 0, 2, 1)
    s2 = jnp.pad(s2, ((0, 0), (0, 0), (0, 0), (0, 3))).reshape(16, 2, ROWS)
    occ = jnp.broadcast_to(occupation.astype(F32)[None, :, None], (16, 2, 128))
    s2 = jnp.concatenate([s2, occ], axis=2).reshape(16, 8, 128)
    o1, o2 = call(
        gather_kernel, (s1, s2),
        (((2, NORB, 768), BF16), ((8, 32, 512), BF16)),
        [pltpu.VMEM((128, 128), F32), pltpu.VMEM((128, 128), F32),
         DMA((8,)), DMA((8,)), DMA((16,)), DMA((16,)), DMA((32,)), DMA((32,)), DMA((8,)), DMA((8,))],
        0, "gather",
    )
    where = jnp.stack([xl * 8 + y * 2 + c, h, z]).astype(jnp.int32)
    v, gp = call(
        potential_kernel,
        (where, o1, o2.reshape(NORB, 512), *permutations(), *tables()),
        (((ROWS, NORB), F32), ((NORB, NORB), F32)),
        [pltpu.VMEM((2, ROWS, 768), F32)],
        name="potential", specs=[SM] + [VM] * 11,
    )
    gram, vs = call(
        reduce_kernel, (gp, v),
        (((NORB, NORB), F32), ((48, NORB), F32)),
        [pltpu.VMEM((32, 8, NORB), F32), pltpu.VMEM((8, 48, NORB), F32), pltpu.VMEM((8, NORB), F32),
         pltpu.VMEM((8, 8, NORB), F32),
         DMA((32,)), DMA((32,)), DMA((8,)), DMA((8,)), DMA((8,)), DMA((8,)), DMA((32,)), DMA((32,))],
        1, "reduce",
    )
    dv, dq = call(
        factor_kernel, (gram, vs),
        (((16, 8, 128), F32), ((16, 8, 128), F32)),
        [pltpu.VMEM((NORB, NORB), F32), pltpu.VMEM((NORB, 128), F32)],
        name="factor",
    )
    ov, oq = call(
        return_kernel, (dv, dq),
        (((2, 48, 128), F32), ((2, 48, 128), F32)),
        [pltpu.VMEM((2, 128, 128), F32), pltpu.VMEM((2, 8, 16, 128), F32), pltpu.VMEM((2, 128, 128), F32),
         DMA((2, 16)), DMA((2, 16)), DMA((2, 8)), DMA((2, 8))],
        2, "give_back",
    )
    return tuple(a[:, :45].reshape(2, HALF) for a in (ov, oq))


def solution(mesh):
    torus = Mesh(mesh.devices.reshape(2, 8, 4, 2, mesh.shape["grid"]), AXES)
    return jax.shard_map(
        on_device,
        mesh=torus,
        in_specs=(P(ORB, "h"), P(ORB)),
        out_specs=(P(ORB, "h"), P(ORB, "h")),
        check_vma=False,
    )
```

time: 784 us -> 95.5 us (0.12); the launches traced: 774 us -> 95.1 us
  waiting for transfers between devices: 471 us -> 0 us
  other arithmetic: 95.2 us -> 0.6 us
  Pallas kernels: 0 us -> 89.1 us
  matrix products: 75.9 us -> 0 us
  local copies, waits for them, and re-layouts: 59.3 us -> 4.7 us
  starting transfers between devices: 38.9 us -> 0 us
  blocking collectives: 16.4 us -> 0 us
  between operations: 16.1 us -> 0.75 us
    psum x1 -> x0, waiting for transfers between devices: 245 us -> none  [on_device(): gram = lax.psum(partial_gram, ORB_GRID)]
    all_gather x1 -> x0, waiting for transfers between devices: 206 us -> none  [in_one_piece(): whole, at, done = (lax.all_gather(both, axis, axis=dim, tiled=True), 0, [])]
    pallas_call x0 -> x5, Pallas kernels: none -> 89.1 us  [call(): pl.pallas_call(kernel, out_shape=[jax.ShapeDtypeStruct(s, d) for s, d in...]
    dot_general x22 -> x0, matrix products: 74.6 us -> none  [the longest x8 31.9 us: solve_pairs(): jnp.einsum('by,pxyz->pxbz', table_y, section, preferred_element_type=jnp....]
    another operation x10 -> x1, other arithmetic: 53.7 us -> 0.6 us  [on_device(): where = jnp.stack([xl * 8 + y * 2 + c, h, z]).astype(jnp.int32)]
    all_to_all x5 -> x0, starting transfers between devices: 38.8 us -> none  [the longest x4 34.5 us: moved_by_axis(): whole = lax.all_to_all(whole, axes[k], k, k, tiled=True)]
    dynamic_slice x12 -> x0, local copies, waits for them, and re-layouts: 22.6 us -> none  [pair_folder(): result, unused = lax.scan(accumulate, running, (blocks, weights))]
    convert_element_type x6 -> x0, other arithmetic: 20.4 us -> none  [the longest x4 19.4 us: accumulate(): (target_rows[:, None, :] * source_rows[None, :, :]).astype(jnp.bfloat16)]
  transfers between devices with their start and end apart: 7 -> 0, of which waited for: 5 -> 0; matrix products, arithmetic and copies ran while one was open for 21% -> 0% of each run, Pallas kernels for 0% -> 0%
where the time goes in v1:
time: 95.5 us; the launch traced here: 95.1 us
  Pallas kernels  89.1 us (93%)
  local copies, waits for them, and re-layouts  4.7 us (5%)
    pallas_call x5, Pallas kernels, call(): pl.pallas_call(kernel, out_shape=[jax.ShapeDtypeStruct(s, d) for s, d in...  89.1 us
    unnamed x10, local copies, waits for them, and re-layouts  2.69 us

profile of v1, /device:TPU:1, one launch (start us, length us, event | category | flops | bytes accessed | tf_op | source)
XLA Modules:
  0.0 95.1 jit_solution(2555904405642354266)
XLA Ops:
  0.6 0.0 copy-start
  0.6 0.0 copy-start.1
  0.7 0.6 pad_add_fusion.where
  1.3 0.1 copy-done.1
  1.3 0.1 broadcast_in_dim.2
  1.4 0.0 copy-done
  1.4 0.2 reshape.32
  1.6 0.2 copy.23
  1.8 0.2 reshape.41
  2.0 0.6 reshape.34.s1
  2.6 0.2 reshape.35
  2.8 0.2 copy.22
  3.0 0.1 reshape.36
  3.2 0.1 copy.20
  3.2 0.7 reshape.37.s2
  3.9 30.0 %gather.1 = (bf16[2,256,768]{2,1,0:T(8,128)(2,1)}, bf16[8,32,512]{2,1,0:T(8,128)(2,1)}) custom-call(f32[8,16,128]{2,1,0:T(8,128)} %reshape.34.s1, f32[16,8,128]{2,1,0:T(8,128)} %reshape.37.s2), custom_call_target="tpu_custom_call" | custom-call | tf_op jit(solution)/shard_map/gather/pallas_call | solution.py:443
  33.9 7.5 %potential.1 = (f32[384,256]{1,0:T(8,128)}, f32[256,256]{1,0:T(8,128)}) custom-call(s32[3]{0:T(128)} %pad_add_fusion.where, bf16[2,256,768]{2,1,0:T(8,128)(2,1)} %get-tuple-element.12.o1, bf16[256,512]{1,0:T(8,128)(2,1)} %bitcast.22, bf16[256,256]{1,0:T(8,128)(2,1)} %constant.45.clone.perm_a, bf16[256,256]{1,0:T(8,128)(2,1)} %constant.46.clone.perm_b, ...), custom_call_target="tpu_custom_call" | custom-call | tf_op jit(solution)/shard_map/potential/pallas_call | solution.py:443
  41.4 28.3 %reduce.1 = (f32[256,256]{1,0:T(8,128)}, f32[48,256]{1,0:T(8,128)}) custom-call(f32[256,256]{1,0:T(8,128)} %get-tuple-element.14.gp, f32[384,256]{1,0:T(8,128)} %get-tuple-element.15.v), custom_call_target="tpu_custom_call" | custom-call | tf_op jit(solution)/shard_map/reduce/pallas_call | solution.py:443
  69.7 8.3 %factor.1 = (f32[16,8,128]{2,1,0:T(8,128)}, f32[16,8,128]{2,1,0:T(8,128)}) custom-call(f32[256,256]{1,0:T(8,128)} %get-tuple-element.16.gram, f32[48,256]{1,0:T(8,128)} %get-tuple-element.17.vs), custom_call_target="tpu_custom_call" | custom-call | tf_op jit(solution)/shard_map/factor/pallas_call | solution.py:443
  77.9 15.1 %give_back.1 = (f32[2,48,128]{2,1,0:T(8,128)}, f32[2,48,128]{2,1,0:T(8,128)}) custom-call(f32[16,8,128]{2,1,0:T(8,128)} %get-tuple-element.18.dv, f32[16,8,128]{2,1,0:T(8,128)} %get-tuple-element.19.dq), custom_call_target="tpu_custom_call" | custom-call | tf_op jit(solution)/shard_map/give_back/pallas_call | solution.py:443
  93.0 0.8 slice_bitcast_fusion
  93.9 0.6 copy.29
  94.5 0.6 copy.30
  (3 shorter events, 0.0 us)
Async XLA Ops:
  0.6 0.7 copy-start
  0.6 0.7 copy-start.1

commit v2 on v1

v2 whole, which is shorter than its diff:
```python
import functools
import math

import jax
import jax.numpy as jnp
import numpy as np
from jax import lax
from jax.experimental import pallas as pl
from jax.experimental.pallas import tpu as pltpu
from jax.sharding import Mesh
from jax.sharding import PartitionSpec as P

NX = 20
NY = 24
NZ = 24
NORB = 256
NPTS = 11520
HALF = NPTS // 2
MODES = 512
ROWS = 384
AXES = ("xl", "z", "y", "c", "h")
ORB = ("xl", "z", "y", "c")
MESH = pl.DeviceIdType.MESH
F32 = jnp.float32
BF16 = jnp.bfloat16


def rounded(a):
    return np.asarray(a, np.float32).astype(jnp.bfloat16).astype(np.float32)


def hartley_table(length):
    index = np.arange(length)
    angle = 2.0 * math.pi / length * (index[:, None] * index[None, :] % length)
    return rounded(np.cos(angle) + np.sin(angle))


def signed_square(length):
    index = np.arange(length)
    signed = np.where(index <= length // 2, index, index - length)
    return (2.0 * math.pi * signed / length) ** 2


def coulomb_kernel():
    total = (
        signed_square(NX)[:, None, None]
        + signed_square(NY)[None, :, None]
        + signed_square(NZ)[None, None, :]
    )
    return np.where(total > 0, 1.0 / np.where(total > 0, total, 1.0), 0.0) / NPTS


def two_parts(a):
    high = rounded(a)
    return high, rounded(a - high)


def tables():
    cx, cy, cz = hartley_table(NX), hartley_table(NY), hartley_table(NZ)
    kernel = coulomb_kernel()
    ac = NX * NZ
    tx = np.zeros((128, MODES), np.float32)
    tx[:NX, :ac] = np.repeat(cx, NZ, axis=1)
    tz = np.zeros((128, MODES), np.float32)
    tz[:NZ, :ac] = np.tile(cz, (1, NX))
    ty = np.zeros((128, 128), np.float32)
    tk = np.zeros((128, MODES), np.float32)
    k_high, k_low = two_parts(kernel.transpose(1, 0, 2).reshape(NY, ac))
    for at, part in ((0, k_high), (32, k_high), (64, k_low)):
        ty[:NY, at : at + NY] = cy
        tk[at : at + NY, :ac] = part
    phi = np.einsum("ax,cz->acxz", cx, cz).reshape(ac, NX, NZ)
    right = np.zeros((MODES, 2, 256), np.float32)
    for h in range(2):
        right[:ac, h, :240] = phi[:, 10 * h : 10 * h + 10].reshape(ac, 240)
    r_high, r_low = two_parts(right.reshape(MODES, 512))
    bf = lambda a: jnp.asarray(a, BF16)
    return bf(tx), bf(tz), bf(ty), bf(tk), bf(r_high), bf(r_low), jnp.asarray(ty[:32], F32)


def permutations():
    true = np.arange(NORB).reshape(2, 8, 8, 2)
    order_a = true.transpose(0, 2, 1, 3).reshape(-1)
    order_b = true.transpose(1, 0, 2, 3).reshape(-1)
    eye = np.eye(NORB, dtype=np.float32)
    return tuple(jnp.asarray(eye[:, o], BF16) for o in (order_a, order_b))


def split2(a):
    high = a.astype(BF16)
    return high, (a - high.astype(F32)).astype(BF16)


def dot(a, b, dims=(1, 0)):
    return lax.dot_general(
        a, b, (((dims[0],), (dims[1],)), ((), ())), preferred_element_type=F32
    )


def me():
    return tuple(lax.axis_index(a) for a in AXES)


def of_plane(pid, z):
    return ((pid // 8) % 2, z, (pid // 2) % 4, pid % 2, pid // 16)


def copy(src, dst, send_sem, recv_sem, device):
    return pltpu.make_async_remote_copy(
        src_ref=src, dst_ref=dst, send_sem=send_sem, recv_sem=recv_sem,
        device_id=device, device_id_type=MESH,
    )


def rows(start, size):
    return pl.ds(pl.multiple_of(start, size), size)


def each(count, body):
    lax.fori_loop(0, count, lambda i, carry: (body(i), carry)[1], 0)


def swap(n, i, body):
    each(n - 1, lambda d: body((i + d + 1) % n))


def greet(barrier, n, i, device):
    swap(n, i, lambda t: pl.semaphore_signal(barrier, inc=1, device_id=device(t), device_id_type=MESH))
    return n - 1


def shifted(a, factor, shift):
    return lax.shift_right_logical(a * factor, shift)


def main_kernel(
    s1, s2, perm_a, perm_b, tx, tz, ty, tk, rh, rl, cy, ov, oq,
    o1, o2, r1, r2, green, left, y_rows, v_f, v_b, gp, gc, gh, rg, rv, s8, rz,
    gram, vall, tt, dd, rp,
    za_s, za_r, pa_s, pa_r, cg_s, cg_r, cf_s, cf_r, zg_s, zg_r,
    gc_s, gc_r, ga_s, ga_r, va_s, va_r, gz_s, gz_r, gg_s, gg_r, gf_s, gf_r,
    vg_s, vg_r, d_s, d_r,
):
    xl, z, y, c, h = me()
    p = xl * 8 + y * 2 + c
    q = h * 8 + xl * 4 + y
    z_dev = lambda t: (xl, t, y, c, h)
    half_dev = lambda t: of_plane(h * 16 + t, z)
    chip_dev = lambda t: ((t // 4) % 2, z, t % 4, c, t // 8)
    core_dev = (xl, z, y, 1 - c, h)

    barrier = pltpu.get_barrier_semaphore()
    greeted = greet(barrier, 8, z, z_dev) + greet(barrier, 16, p, half_dev)
    greeted += greet(barrier, 16, q, chip_dev)
    pl.semaphore_signal(barrier, inc=1, device_id=core_dev, device_id_type=MESH)

    row = lax.broadcasted_iota(jnp.int32, (ROWS, 128), 0)
    lane = lax.broadcasted_iota(jnp.int32, (ROWS, 128), 1)
    zz = shifted(row, 1366, 16)
    s = row - zz * 48
    cell = h * HALF + s * 128 + zz * 16 + p
    x = shifted(cell, 7282, 22)
    yz = cell - x * (NY * NZ)
    y_cell = shifted(yz, 2731, 16)
    z_cell = yz - y_cell * NZ
    hot = lambda a: jnp.where(a == lane, 1.0, 0.0).astype(BF16)
    left[...] = dot(hot(jnp.where(s < 45, x, 127)), tx[...]) * dot(hot(z_cell), tz[...])
    y_rows[...] = dot(hot(y_cell), ty[...])
    middle = (lane >= 32) & (lane < 64)

    def green_part(t):
        k_high, k_low = split2(y_rows[...] * cy[pl.ds(z * 3 + t, 1), :])
        mix = jnp.where(middle, k_low.astype(F32), k_high.astype(F32)).astype(BF16)
        l_high, l_low = split2(left[...] * dot(mix, tk[...]))
        g = dot(l_high, rh[...]) + dot(l_low, rh[...]) + dot(l_high, rl[...])
        for hh in range(2):
            green[hh, :, t * 256 : (t + 1) * 256] = g[:, hh * 256 : (hh + 1) * 256]

    pl.semaphore_wait(barrier, greeted + 1)

    def z_send(t):
        return copy(s1.at[t], r1.at[rows(z * 16, 16)], za_s.at[t], za_r.at[z], z_dev(t))

    def z_recv(t):
        return copy(s1.at[t], r1.at[rows(t * 16, 16)], za_s.at[t], za_r.at[t], z_dev(t))

    def p_send(t):
        return copy(s2.at[t], r2.at[rows(p * 8, 8)], pa_s.at[t], pa_r.at[p], half_dev(t))

    def p_recv(t):
        return copy(s2.at[t], r2.at[rows(t * 8, 8)], pa_s.at[t], pa_r.at[t], half_dev(t))

    swap(8, z, lambda t: z_send(t).start())
    swap(16, p, lambda t: p_send(t).start())
    r1[rows(z * 16, 16)] = s1[z]
    r2[rows(p * 8, 8)] = s2[p]
    green_part(0)
    swap(8, z, lambda t: z_recv(t).wait_recv())
    for t in range(3):
        o1[h, rows(p * 16, 16), t * 256 : (t + 1) * 256] = jnp.concatenate(
            [r1[pl.ds(2 * t + k, 16, stride=8), :] for k in range(2)], axis=1
        ).astype(BF16)

    def block(t, core):
        return o1.at[t // 8, rows(((t // 4) % 2 * 8 + t % 4 * 2 + core) * 16, 16)]

    def c_send(t):
        return copy(block(q, c), block(q, c), cg_s.at[t], cg_r.at[q], chip_dev(t))

    def c_recv(t):
        return copy(block(t, c), block(t, c), cg_s.at[t], cg_r.at[t], chip_dev(t))

    def f_send(t):
        return copy(block(t, c), block(t, c), cf_s.at[t], cf_r.at[t], core_dev)

    def f_recv(t):
        return copy(block(t, 1 - c), block(t, 1 - c), cf_s.at[t], cf_r.at[t], core_dev)

    swap(16, q, lambda t: c_send(t).start())
    f_send(q).start()
    swap(16, p, lambda t: p_recv(t).wait_recv())
    for k in range(3):
        o2[rows(z * 32, 32), k * 128 : (k + 1) * 128] = r2[pl.ds(k, 32, stride=4), :].astype(BF16)

    def zg_send(t):
        mine = o2.at[rows(z * 32, 32)]
        return copy(mine, mine, zg_s.at[t], zg_r.at[z], z_dev(t))

    def zg_recv(t):
        theirs = o2.at[rows(t * 32, 32)]
        return copy(theirs, theirs, zg_s.at[t], zg_r.at[t], z_dev(t))

    swap(8, z, lambda t: zg_send(t).start())
    green_part(1)
    green_part(2)

    def pass_on(t):
        c_recv(t).wait_recv()
        f_send(t).start()

    swap(16, q, pass_on)
    swap(8, z, lambda t: zg_recv(t).wait_recv())
    o_rows = dot(perm_b[...], o2[...])
    o_b = o_rows.astype(BF16)
    w = (o_rows * o_rows[:, 45:46]).astype(BF16).T
    each(16, lambda t: f_recv(t).wait_recv())

    v = jnp.zeros((NORB, ROWS), F32)
    for hh in range(2):
        orb = dot(perm_a[...], o1[hh]).astype(BF16)
        m_high, m_low = split2(green[hh] * dot(w, orb))
        v = v + dot(orb, m_high, (1, 1)) + dot(orb, m_low, (1, 1))
    v_high, v_low = split2(v)
    gp[...] = (dot(o_b, v_high, (1, 1)) + dot(o_b, v_low, (1, 1))) * (1.0 / NPTS)

    def half_send():
        other = gp.at[rows((1 - c) * 128, 128)]
        return copy(other, gc, gc_s, gc_r, core_dev)

    def v_part(part, t):
        return v_b.at[part, :, rows(t * 16, 16), :]

    def v_send(part, t):
        return copy(v_part(part, t), rv.at[part, z], va_s.at[part, t], va_r.at[part, z], z_dev(t))

    def v_recv(part, t):
        return copy(v_part(part, t), rv.at[part, t], va_s.at[part, t], va_r.at[part, t], z_dev(t))

    half_send().start()
    for part, value in ((0, v_high), (1, v_low)):
        v_b[part] = value.reshape(2, 128, ROWS)
    v_f[...] = v.reshape(2, 128, ROWS)
    swap(8, z, lambda t: v_send(0, t).start())
    half_send().wait_recv()
    gh[...] = gp[rows(c * 128, 128)] + gc[...]

    def a_send(t):
        return copy(gh.at[rows(t * 8, 8)], rg.at[q], ga_s.at[t], ga_r.at[q], chip_dev(t))

    def a_recv(t):
        return copy(gh.at[rows(t * 8, 8)], rg.at[t], ga_s.at[t], ga_r.at[t], chip_dev(t))

    swap(16, q, lambda t: a_send(t).start())
    rg[q] = gh[rows(q * 8, 8)]
    for part in range(2):
        rv[part, z] = jnp.zeros((2, 16, ROWS), BF16)
    swap(16, q, lambda t: a_recv(t).wait_recv())
    s8[...] = jnp.sum(rg[...], axis=0)

    def gz_send(t):
        return copy(s8, rz.at[z], gz_s.at[t], gz_r.at[z], z_dev(t))

    def gz_recv(t):
        return copy(s8, rz.at[t], gz_s.at[t], gz_r.at[t], z_dev(t))

    swap(8, z, lambda t: gz_send(t).start())
    swap(8, z, lambda t: v_send(1, t).start())
    rz[z] = s8[...]
    swap(8, z, lambda t: gz_recv(t).wait_recv())

    def line(t, core):
        return gram.at[rows(core * 128 + t * 8, 8)]

    gram[rows(c * 128 + q * 8, 8)] = jnp.sum(rz[...], axis=0)

    def g_send(t):
        return copy(line(q, c), line(q, c), gg_s.at[t], gg_r.at[q], chip_dev(t))

    def g_recv(t):
        return copy(line(t, c), line(t, c), gg_s.at[t], gg_r.at[t], chip_dev(t))

    def gf_send(t):
        return copy(line(t, c), line(t, c), gf_s.at[t], gf_r.at[t], core_dev)

    def gf_recv(t):
        return copy(line(t, 1 - c), line(t, 1 - c), gf_s.at[t], gf_r.at[t], core_dev)

    swap(16, q, lambda t: g_send(t).start())
    gf_send(q).start()

    for part in range(2):
        swap(8, z, lambda t, part=part: v_recv(part, t).wait_recv())
    others = jnp.sum(rv[0].astype(F32) + rv[1].astype(F32), axis=0)
    mine = -(v_f[:, rows(z * 16, 16), :] + others)
    m_high, m_low = split2(mine)
    own = vall.at[:, rows(z * 16, 16), :]
    own[:, :, :ROWS] = m_high
    own[:, :, ROWS:] = m_low

    def vg_send(t):
        return copy(own, own, vg_s.at[t], vg_r.at[z], z_dev(t))

    def vg_recv(t):
        theirs = vall.at[:, rows(t * 16, 16), :]
        return copy(theirs, theirs, vg_s.at[t], vg_r.at[t], z_dev(t))

    swap(8, z, lambda t: vg_send(t).start())

    def g_pass_on(t):
        g_recv(t).wait_recv()
        gf_send(t).start()

    swap(16, q, g_pass_on)

    def d_send(n, t):
        return copy(dd.at[n, rows(t * 8, 8)], rp.at[n, rows(p * 8, 8)], d_s.at[n, t], d_r.at[n, p], half_dev(t))

    def d_recv(n, t):
        return copy(dd.at[n, rows(t * 8, 8)], rp.at[n, rows(t * 8, 8)], d_s.at[n, t], d_r.at[n, t], half_dev(t))

    def deal(n, value):
        for k in range(3):
            tt[n, k] = value[:, k * 128 : (k + 1) * 128]
        even, odd = (
            jnp.concatenate([tt[n, k, pl.ds(o, 16, stride=2), :] for k in range(3)], axis=1)
            for o in range(2)
        )
        gap = jnp.zeros((16, 16), F32)
        for k in range(8):
            cells = slice(48 * k, 48 * k + 48)
            dd[n, pl.ds(k, 16, stride=8), :] = jnp.concatenate(
                [even[:, cells], gap, odd[:, cells], gap], axis=1
            )
        swap(16, p, lambda t: d_send(n, t).start())
        rp[n, rows(p * 8, 8)] = dd[n, rows(p * 8, 8)]

    def land(n, out):
        swap(16, p, lambda t: d_recv(n, t).wait_recv())
        table = jnp.concatenate([rp[n, pl.ds(k, 16, stride=8), :] for k in range(8)], axis=0)
        turned = table.T
        for k in range(45):
            out[:, k * 128 : (k + 1) * 128] = jnp.concatenate(
                [turned[k : k + 1], turned[64 + k : 65 + k]], axis=0
            )

    deal(0, mine.reshape(32, ROWS))
    each(16, lambda t: gf_recv(t).wait_recv())
    half_send().wait_send()
    swap(16, q, lambda t: g_send(t).wait_send())
    each(16, lambda t: gf_send(t).wait_send())
    a = gram[...]
    gram[...] = (a + a.T) * 0.5
    eliminate(gram)
    l_rows = jnp.concatenate([gram[rows(k * 128 + z * 16, 16), :] for k in range(2)], axis=0)
    l_both = jnp.concatenate(split2(l_rows), axis=0)
    swap(8, z, lambda t: vg_recv(t).wait_recv())
    out = dot(l_both, vall[...].reshape(NORB, 2 * ROWS))
    deal(1, out[:32, :ROWS] + out[32:, :ROWS] + out[:32, ROWS:])
    land(0, ov)
    for group, i, sends in (
        (8, z, (z_send, zg_send, functools.partial(v_send, 0), functools.partial(v_send, 1), gz_send, vg_send)),
        (16, p, (p_send, functools.partial(d_send, 0))),
        (16, q, (c_send, a_send)),
    ):
        for send in sends:
            swap(group, i, lambda t, send=send: send(t).wait_send())
    each(16, lambda t: f_send(t).wait_send())
    land(1, oq)
    swap(16, p, lambda t: d_send(1, t).wait_send())


def eliminate(work):
    sub = lax.broadcasted_iota(jnp.int32, (8, 128), 0)
    lane = lax.broadcasted_iota(jnp.int32, (8, 128), 1)
    wide = lambda col: jnp.broadcast_to(col, (8, 128))
    for k in range(8):
        base = 32 * k
        tile, off = base // 128, base % 128
        wk = [
            [work[base + 8 * g : base + 8 * g + 8, 128 * t : 128 * t + 128] for t in range(2)]
            for g in range(4)
        ]
        col = [
            [wide(wk[g][tile][:, off + j : off + j + 1]) if g >= j // 8 else None for g in range(4)]
            for j in range(32)
        ]
        inside = (lane >= off) & (lane < off + 32)
        for g in range(4):
            unit = jnp.where(lane - off == sub + 8 * g, 1.0, 0.0)
            wk[g][tile] = jnp.where(inside, unit, wk[g][tile])
        pivots = [jnp.ones((8, 128), F32) for _ in range(4)]
        for j in range(0, 32, 2):
            gj, sj = j // 8, j % 8
            u, v = col[j], col[j + 1]
            p11 = wide(u[gj][sj : sj + 1, :])
            p21 = wide(u[gj][sj + 1 : sj + 2, :])
            p22 = wide(v[gj][sj + 1 : sj + 2, :])
            det = p11 * p22 - p21 * p21
            r = 1.0 / det
            r11 = 1.0 / p11
            pivots[gj] = jnp.where(sub == sj, p11, jnp.where(sub == sj + 1, det * r11, pivots[gj]))
            q11, q21, q22 = p22 * r, p21 * r, p11 * r
            al, be = [None] * 4, [None] * 4
            for g in range(gj, 4):
                al[g] = u[g] * q11 - v[g] * q21
                be[g] = v[g] * q22 - u[g] * q21
            below = sub > sj + 1
            be[gj] = jnp.where(below, be[gj], 0.0)
            al[gj] = jnp.where(below, al[gj], jnp.where(sub == sj + 1, p21 * r11, 0.0))
            for i in range(j + 2, 32):
                fu = wide(u[i // 8][i % 8 : i % 8 + 1, :])
                fv = wide(v[i // 8][i % 8 : i % 8 + 1, :])
                for g in range(i // 8, 4):
                    col[i][g] = col[i][g] - (al[g] * fu + be[g] * fv)
            for t in range(2):
                one = wide(wk[gj][t][sj : sj + 1, :])
                two = wide(wk[gj][t][sj + 1 : sj + 2, :])
                for g in range(gj, 4):
                    wk[g][t] = wk[g][t] - (al[g] * one + be[g] * two)
        for g in range(4):
            scale = lax.rsqrt(pivots[g])
            for t in range(2):
                wk[g][t] = wk[g][t] * scale
        u = jnp.concatenate([jnp.concatenate(wk[g], axis=1) for g in range(4)], axis=0)
        lanes = lax.broadcasted_iota(jnp.int32, (32, 256), 1)
        work[base : base + 32, :] = jnp.where(lanes < base + 32, u, 0.0)
        if k < 7:
            u_high, u_low = split2(u)
            one = jnp.concatenate([u_high, u_low, u_high], axis=0)
            two = jnp.concatenate([u_high, u_high, u_low], axis=0)
            edge = base + 32
            start = edge // 128 * 128
            change = dot(one[:, start:].T, two)[edge - start :]
            rest = work[edge:, :]
            lanes = lax.broadcasted_iota(jnp.int32, rest.shape, 1)
            rest = jnp.where((lanes >= base) & (lanes < edge), 0.0, rest)
            work[edge:, :] = rest - change


VM = pl.BlockSpec(memory_space=pltpu.VMEM)
SM = pl.BlockSpec(memory_space=pltpu.SMEM)
DMA = pltpu.SemaphoreType.DMA


def call(kernel, args, outs, scratch, number=None, name=None, specs=None):
    params = dict(vmem_limit_bytes=60 * 1024 * 1024)
    if number is not None:
        params.update(collective_id=number, has_side_effects=True)
    return pl.pallas_call(
        kernel,
        out_shape=[jax.ShapeDtypeStruct(s, d) for s, d in outs],
        in_specs=specs or [VM] * len(args),
        out_specs=[VM] * len(outs),
        scratch_shapes=scratch,
        compiler_params=pltpu.CompilerParams(**params),
        name=name,
    )(*args)


def on_device(orbitals, occupation):
    xl, z, y, c, h = me()
    own = orbitals.astype(F32)
    s1 = own.reshape(2, 10, 8, 3, NZ).transpose(2, 0, 3, 1, 4).reshape(8, 2, 3, 240)
    s1 = jnp.pad(s1, ((0, 0), (0, 0), (0, 1), (0, 16))).reshape(8, 16, 128)
    s2 = own.reshape(2, 45, 8, 16).transpose(3, 0, 2, 1)
    occ = jnp.broadcast_to(occupation.astype(F32)[None, :, None, None], (16, 2, 8, 1))
    s2 = jnp.concatenate([s2, occ], axis=3)
    s2 = jnp.pad(s2, ((0, 0), (0, 0), (0, 0), (0, 2))).reshape(16, 2, ROWS)
    s2 = jnp.pad(s2, ((0, 0), (0, 0), (0, 128))).reshape(16, 8, 128)
    vm = pltpu.VMEM
    return tuple(call(
        main_kernel, (s1, s2, *permutations(), *tables()),
        (((2, HALF), F32), ((2, HALF), F32)),
        [vm((2, NORB, 768), BF16), vm((NORB, ROWS), BF16), vm((128, 128), F32), vm((128, 128), F32),
         vm((2, ROWS, 768), F32), vm((ROWS, MODES), F32), vm((ROWS, 128), F32),
         vm((2, 128, ROWS), F32), vm((2, 2, 128, ROWS), BF16), vm((NORB, NORB), F32),
         vm((128, NORB), F32), vm((128, NORB), F32), vm((16, 8, NORB), F32),
         vm((2, 8, 2, 16, ROWS), BF16), vm((8, NORB), F32), vm((8, 8, NORB), F32),
         vm((NORB, NORB), F32), vm((2, 128, 2 * ROWS), BF16), vm((2, 3, 32, 128), F32),
         vm((2, 128, 128), F32), vm((2, 128, 128), F32),
         DMA((8,)), DMA((8,)), DMA((16,)), DMA((16,)), DMA((16,)), DMA((16,)), DMA((16,)), DMA((16,)),
         DMA((8,)), DMA((8,)), DMA, DMA, DMA((16,)), DMA((16,)), DMA((2, 8)), DMA((2, 8)),
         DMA((8,)), DMA((8,)), DMA((16,)), DMA((16,)), DMA((16,)), DMA((16,)),
         DMA((8,)), DMA((8,)), DMA((2, 16)), DMA((2, 16))],
        0, "exchange",
    ))


def solution(mesh):
    torus = Mesh(mesh.devices.reshape(2, 8, 4, 2, mesh.shape["grid"]), AXES)
    return jax.shard_map(
        on_device,
        mesh=torus,
        in_specs=(P(ORB, "h"), P(ORB)),
        out_specs=(P(ORB, "h"), P(ORB, "h")),
        check_vma=False,
    )
```

time: 95.5 us -> 68 us (0.71)
  Pallas kernels: 89.1 us -> 60.9 us
  local copies, waits for them, and re-layouts: 4.7 us -> 5.95 us
    pallas_call x5 -> x1, Pallas kernels: 89.1 us -> 60.9 us  [call(): pl.pallas_call(kernel, out_shape=[jax.ShapeDtypeStruct(s, d) for s, d in...]
where the time goes in v2:
time: 68 us; the launch traced here: 67.7 us
  Pallas kernels  60.9 us (90%)
  local copies, waits for them, and re-layouts  5.95 us (9%)
  between operations  0.71 us (1%)
    pallas_call x1, Pallas kernels, call(): pl.pallas_call(kernel, out_shape=[jax.ShapeDtypeStruct(s, d) for s, d in...  60.9 us
    unnamed x10, local copies, waits for them, and re-layouts  3.02 us

profile of v2, /device:TPU:1, one launch (start us, length us, event | category | flops | bytes accessed | tf_op | source)
XLA Modules:
  0.0 67.7 jit_solution(11367266287394699360)
XLA Ops:
  0.6 1.0 %reshape.25 = f32[2,10,8,3,24]{4,3,2,1,0:T(4,128)S(1)} reshape(bf16[2,5760]{1,0:T(2,128)(2,1)} %param.11) | data formatting | bytes 69120 | tf_op jit(solution)/shard_map/reshape | solution.py:493
  1.6 0.2 copy.29
  1.8 0.2 reshape.32
  2.0 0.0 copy-start.2
  2.0 0.6 reshape.27.s1
  2.6 0.0 copy-done.2
  2.6 0.0 copy-start
  2.6 0.1 broadcast_in_dim.2
  2.7 0.7 copy-done
  3.4 0.2 reshape.28
  3.5 0.2 copy.23
  3.8 0.1 select_maximum_fusion
  3.9 0.1 reshape.31
  4.0 0.7 reshape.30.s2
  4.7 60.9 %exchange.1 = (f32[2,5760]{1,0:T(2,128)}, f32[2,5760]{1,0:T(2,128)}) custom-call(f32[8,16,128]{2,1,0:T(8,128)} %reshape.27.s1, f32[16,8,128]{2,1,0:T(8,128)} %reshape.30.s2, bf16[256,256]{1,0:T(8,128)(2,1)} %constant.21.clone.perm_a, bf16[256,256]{1,0:T(8,128)(2,1)} %constant.22.clone.perm_b, bf16[128,512]{1,0:T(8,128)(2,1)} %constant.23.clone.tx, ...), custom_call_target="tpu_custom_call" | custom-call | tf_op jit(solution)/shard_map/exchange/pallas_call | solution.py:479
  65.6 0.0 copy-start.1
  65.6 1.4 %copy.33 = f32[2,5760]{1,0:T(2,128)} copy(f32[2,5760]{1,0:T(2,128)} %get-tuple-element.4) | data formatting | bytes 92160
  67.1 0.0 copy-done.1
  67.1 0.6 copy.34
  (2 shorter events, 0.0 us)
Async XLA Ops:
  2.0 0.7 copy-start.2
  2.6 0.7 %copy-start = (bf16[2,5760]{1,0:T(2,128)(2,1)S(1)}, bf16[2,5760]{1,0:T(2,128)(2,1)}, u32[]{:S(2)}) copy-start(bf16[2,5760]{1,0:T(2,128)(2,1)} %param.11) | copy-start | bytes 69124
  65.6 1.4 %copy-start.1 = (f32[2,5760]{1,0:T(2,128)S(1)}, f32[2,5760]{1,0:T(2,128)}, u32[]{:S(2)}) copy-start(f32[2,5760]{1,0:T(2,128)} %get-tuple-element.5) | copy-start | bytes 138244

commit v3 on v2

--- a/solution.py
+++ b/solution.py
@@ -75,7 +75,8 @@
         right[:ac, h, :240] = phi[:, 10 * h : 10 * h + 10].reshape(ac, 240)
     r_high, r_low = two_parts(right.reshape(MODES, 512))
     bf = lambda a: jnp.asarray(a, BF16)
-    return bf(tx), bf(tz), bf(ty), bf(tk), bf(r_high), bf(r_low), jnp.asarray(ty[:32], F32)
+    three = np.concatenate([tx, tz, tk], axis=1)
+    return bf(three), bf(ty), bf(np.concatenate([r_high, r_low], axis=1)), jnp.asarray(ty[:32], F32)
 
 
 def permutations():
@@ -83,7 +84,7 @@
     order_a = true.transpose(0, 2, 1, 3).reshape(-1)
     order_b = true.transpose(1, 0, 2, 3).reshape(-1)
     eye = np.eye(NORB, dtype=np.float32)
-    return tuple(jnp.asarray(eye[:, o], BF16) for o in (order_a, order_b))
+    return jnp.asarray(np.concatenate([eye[:, order_a], eye[:, order_b]], axis=1), BF16)
 
 
 def split2(a):
@@ -124,6 +125,14 @@
     each(n - 1, lambda d: body((i + d + 1) % n))
 
 
+Z_ORDER = (4, 3, 5, 2, 6, 1, 7)
+CHIP_ORDER = (
+    (2, 2), (2, 1), (2, 3), (1, 2), (3, 2), (1, 1), (1, 3), (3, 1), (3, 3),
+    (2, 0), (0, 2), (1, 0), (3, 0), (0, 1), (0, 3),
+)
+HALF_ORDER = tuple((a, b, k) for a, b in ((1, 2), (1, 1), (1, 3), (0, 2), (1, 0), (0, 1), (0, 3)) for k in range(2)) + ((0, 0, 1),)
+
+
 def greet(barrier, n, i, device):
     swap(n, i, lambda t: pl.semaphore_signal(barrier, inc=1, device_id=device(t), device_id_type=MESH))
     return n - 1
@@ -134,7 +143,8 @@
 
 
 def main_kernel(
-    s1, s2, perm_a, perm_b, tx, tz, ty, tk, rh, rl, cy, ov, oq,
+    s1_any, s2_any, perm_any, t_any, ty_any, right_any, cy_any, ov, oq,
+    s1, s2, perm, t3, ty, right, cy, in_s,
     o1, o2, r1, r2, green, left, y_rows, v_f, v_b, gp, gc, gh, rg, rv, s8, rz,
     gram, vall, tt, dd, rp,
     za_s, za_r, pa_s, pa_r, cg_s, cg_r, cf_s, cf_r, zg_s, zg_r,
@@ -149,10 +159,35 @@
     chip_dev = lambda t: ((t // 4) % 2, z, t % 4, c, t // 8)
     core_dev = (xl, z, y, 1 - c, h)
 
+    def z_line(body):
+        for d in Z_ORDER:
+            body((z + d) % 8)
+
+    def chips(body):
+        for dx, dy in CHIP_ORDER:
+            body((q // 4 + dx) % 4 * 4 + (y + dy) % 4)
+
+    def half(body):
+        for dx, dy, dc in HALF_ORDER:
+            body((xl + dx) % 2 * 8 + (y + dy) % 4 * 2 + (c + dc) % 2)
+
     barrier = pltpu.get_barrier_semaphore()
     greeted = greet(barrier, 8, z, z_dev) + greet(barrier, 16, p, half_dev)
     greeted += greet(barrier, 16, q, chip_dev)
     pl.semaphore_signal(barrier, inc=1, device_id=core_dev, device_id_type=MESH)
+
+    held = (
+        (s1_any, s1), (s2_any, s2), (t_any, t3), (ty_any, ty), (cy_any, cy),
+        (right_any, right), (perm_any, perm),
+    )
+    held = [pltpu.make_async_copy(a, b, in_s.at[k]) for k, (a, b) in enumerate(held)]
+    for one in held:
+        one.start()
+    perm_a, perm_b = perm.at[:, :NORB], perm.at[:, NORB:]
+    tx, tz, tk = (t3.at[:, k * MODES : (k + 1) * MODES] for k in range(3))
+    rh, rl = right.at[:, :512], right.at[:, 512:]
+    for one in held[2:5]:
+        one.wait()
 
     row = lax.broadcasted_iota(jnp.int32, (ROWS, 128), 0)
     lane = lax.broadcasted_iota(jnp.int32, (ROWS, 128), 1)
@@ -176,6 +211,8 @@
         for hh in range(2):
             green[hh, :, t * 256 : (t + 1) * 256] = g[:, hh * 256 : (hh + 1) * 256]
 
+    for one in held[:2]:
+        one.wait()
     pl.semaphore_wait(barrier, greeted + 1)
 
     def z_send(t):
@@ -190,11 +227,26 @@
     def p_recv(t):
         return copy(s2.at[t], r2.at[rows(t * 8, 8)], pa_s.at[t], pa_r.at[t], half_dev(t))
 
-    swap(8, z, lambda t: z_send(t).start())
-    swap(16, p, lambda t: p_send(t).start())
+    half(lambda t: p_send(t).start())
+    z_line(lambda t: z_send(t).start())
     r1[rows(z * 16, 16)] = s1[z]
     r2[rows(p * 8, 8)] = s2[p]
+    for one in held[5:]:
+        one.wait()
     green_part(0)
+    swap(16, p, lambda t: p_recv(t).wait_recv())
+    for k in range(3):
+        o2[rows(z * 32, 32), k * 128 : (k + 1) * 128] = r2[pl.ds(k, 32, stride=4), :].astype(BF16)
+
+    def zg_send(t):
+        mine = o2.at[rows(z * 32, 32)]
+        return copy(mine, mine, zg_s.at[t], zg_r.at[z], z_dev(t))
+
+    def zg_recv(t):
+        theirs = o2.at[rows(t * 32, 32)]
+        return copy(theirs, theirs, zg_s.at[t], zg_r.at[t], z_dev(t))
+
+    z_line(lambda t: zg_send(t).start())
     swap(8, z, lambda t: z_recv(t).wait_recv())
     for t in range(3):
         o1[h, rows(p * 16, 16), t * 256 : (t + 1) * 256] = jnp.concatenate(
@@ -216,21 +268,8 @@
     def f_recv(t):
         return copy(block(t, 1 - c), block(t, 1 - c), cf_s.at[t], cf_r.at[t], core_dev)
 
-    swap(16, q, lambda t: c_send(t).start())
+    chips(lambda t: c_send(t).start())
     f_send(q).start()
-    swap(16, p, lambda t: p_recv(t).wait_recv())
-    for k in range(3):
-        o2[rows(z * 32, 32), k * 128 : (k + 1) * 128] = r2[pl.ds(k, 32, stride=4), :].astype(BF16)
-
-    def zg_send(t):
-        mine = o2.at[rows(z * 32, 32)]
-        return copy(mine, mine, zg_s.at[t], zg_r.at[z], z_dev(t))
-
-    def zg_recv(t):
-        theirs = o2.at[rows(t * 32, 32)]
-        return copy(theirs, theirs, zg_s.at[t], zg_r.at[t], z_dev(t))
-
-    swap(8, z, lambda t: zg_send(t).start())
     green_part(1)
     green_part(2)
 
@@ -238,7 +277,7 @@
         c_recv(t).wait_recv()
         f_send(t).start()
 
-    swap(16, q, pass_on)
+    chips(pass_on)
     swap(8, z, lambda t: zg_recv(t).wait_recv())
     o_rows = dot(perm_b[...], o2[...])
     o_b = o_rows.astype(BF16)
@@ -257,20 +296,26 @@
         other = gp.at[rows((1 - c) * 128, 128)]
         return copy(other, gc, gc_s, gc_r, core_dev)
 
-    def v_part(part, t):
-        return v_b.at[part, :, rows(t * 16, 16), :]
-
     def v_send(part, t):
-        return copy(v_part(part, t), rv.at[part, z], va_s.at[part, t], va_r.at[part, z], z_dev(t))
+        if part == 0:
+            src, dst = v_b.at[0, :, rows(t * 16, 16), :], rv.at[0, z]
+        else:
+            src, dst = v_b.at[1, part - 1, rows(t * 16, 16), :], rv.at[1, z, part - 1]
+        return copy(src, dst, va_s.at[part, t], va_r.at[part, z], z_dev(t))
 
     def v_recv(part, t):
-        return copy(v_part(part, t), rv.at[part, t], va_s.at[part, t], va_r.at[part, t], z_dev(t))
+        if part == 0:
+            src, dst = v_b.at[0, :, rows(t * 16, 16), :], rv.at[0, t]
+        else:
+            src, dst = v_b.at[1, part - 1, rows(t * 16, 16), :], rv.at[1, t, part - 1]
+        return copy(src, dst, va_s.at[part, t], va_r.at[part, t], z_dev(t))
 
     half_send().start()
     for part, value in ((0, v_high), (1, v_low)):
         v_b[part] = value.reshape(2, 128, ROWS)
     v_f[...] = v.reshape(2, 128, ROWS)
-    swap(8, z, lambda t: v_send(0, t).start())
+    z_line(lambda t: v_send(0, t).start())
+    z_line(lambda t: v_send(1, t).start())
     half_send().wait_recv()
     gh[...] = gp[rows(c * 128, 128)] + gc[...]
 
@@ -280,7 +325,7 @@
     def a_recv(t):
         return copy(gh.at[rows(t * 8, 8)], rg.at[t], ga_s.at[t], ga_r.at[t], chip_dev(t))
 
-    swap(16, q, lambda t: a_send(t).start())
+    chips(lambda t: a_send(t).start())
     rg[q] = gh[rows(q * 8, 8)]
     for part in range(2):
         rv[part, z] = jnp.zeros((2, 16, ROWS), BF16)
@@ -293,8 +338,8 @@
     def gz_recv(t):
         return copy(s8, rz.at[t], gz_s.at[t], gz_r.at[t], z_dev(t))
 
-    swap(8, z, lambda t: gz_send(t).start())
-    swap(8, z, lambda t: v_send(1, t).start())
+    z_line(lambda t: gz_send(t).start())
+    z_line(lambda t: v_send(2, t).start())
     rz[z] = s8[...]
     swap(8, z, lambda t: gz_recv(t).wait_recv())
 
@@ -315,10 +360,10 @@
     def gf_recv(t):
         return copy(line(t, 1 - c), line(t, 1 - c), gf_s.at[t], gf_r.at[t], core_dev)
 
-    swap(16, q, lambda t: g_send(t).start())
+    chips(lambda t: g_send(t).start())
     gf_send(q).start()
 
-    for part in range(2):
+    for part in range(3):
         swap(8, z, lambda t, part=part: v_recv(part, t).wait_recv())
     others = jnp.sum(rv[0].astype(F32) + rv[1].astype(F32), axis=0)
     mine = -(v_f[:, rows(z * 16, 16), :] + others)
@@ -334,13 +379,13 @@
         theirs = vall.at[:, rows(t * 16, 16), :]
         return copy(theirs, theirs, vg_s.at[t], vg_r.at[t], z_dev(t))
 
-    swap(8, z, lambda t: vg_send(t).start())
+    z_line(lambda t: vg_send(t).start())
 
     def g_pass_on(t):
         g_recv(t).wait_recv()
         gf_send(t).start()
 
-    swap(16, q, g_pass_on)
+    chips(g_pass_on)
 
     def d_send(n, t):
         return copy(dd.at[n, rows(t * 8, 8)], rp.at[n, rows(p * 8, 8)], d_s.at[n, t], d_r.at[n, p], half_dev(t))
@@ -361,7 +406,7 @@
             dd[n, pl.ds(k, 16, stride=8), :] = jnp.concatenate(
                 [even[:, cells], gap, odd[:, cells], gap], axis=1
             )
-        swap(16, p, lambda t: d_send(n, t).start())
+        half(lambda t: d_send(n, t).start())
         rp[n, rows(p * 8, 8)] = dd[n, rows(p * 8, 8)]
 
     def land(n, out):
@@ -388,7 +433,7 @@
     deal(1, out[:32, :ROWS] + out[32:, :ROWS] + out[:32, ROWS:])
     land(0, ov)
     for group, i, sends in (
-        (8, z, (z_send, zg_send, functools.partial(v_send, 0), functools.partial(v_send, 1), gz_send, vg_send)),
+        (8, z, (z_send, zg_send, *(functools.partial(v_send, k) for k in range(3)), gz_send, vg_send)),
         (16, p, (p_send, functools.partial(d_send, 0))),
         (16, q, (c_send, a_send)),
     ):
@@ -468,21 +513,20 @@
 
 
 VM = pl.BlockSpec(memory_space=pltpu.VMEM)
-SM = pl.BlockSpec(memory_space=pltpu.SMEM)
+ANY = pl.BlockSpec(memory_space=pl.ANY)
 DMA = pltpu.SemaphoreType.DMA
 
 
-def call(kernel, args, outs, scratch, number=None, name=None, specs=None):
-    params = dict(vmem_limit_bytes=60 * 1024 * 1024)
-    if number is not None:
-        params.update(collective_id=number, has_side_effects=True)
+def call(kernel, args, outs, scratch, number, name):
     return pl.pallas_call(
         kernel,
         out_shape=[jax.ShapeDtypeStruct(s, d) for s, d in outs],
-        in_specs=specs or [VM] * len(args),
+        in_specs=[ANY] * len(args),
         out_specs=[VM] * len(outs),
         scratch_shapes=scratch,
-        compiler_params=pltpu.CompilerParams(**params),
+        compiler_params=pltpu.CompilerParams(
+            vmem_limit_bytes=60 * 1024 * 1024, collective_id=number, has_side_effects=True
+        ),
         name=name,
     )(*args)
 
@@ -499,9 +543,11 @@
     s2 = jnp.pad(s2, ((0, 0), (0, 0), (0, 128))).reshape(16, 8, 128)
     vm = pltpu.VMEM
     return tuple(call(
-        main_kernel, (s1, s2, *permutations(), *tables()),
+        main_kernel, (s1, s2, permutations(), *tables()),
         (((2, HALF), F32), ((2, HALF), F32)),
-        [vm((2, NORB, 768), BF16), vm((NORB, ROWS), BF16), vm((128, 128), F32), vm((128, 128), F32),
+        [vm((8, 16, 128), F32), vm((16, 8, 128), F32), vm((NORB, 512), BF16), vm((128, 3 * MODES), BF16),
+         vm((128, 128), BF16), vm((MODES, 1024), BF16), vm((32, 128), F32), DMA((7,)),
+         vm((2, NORB, 768), BF16), vm((NORB, ROWS), BF16), vm((128, 128), F32), vm((128, 128), F32),
          vm((2, ROWS, 768), F32), vm((ROWS, MODES), F32), vm((ROWS, 128), F32),
          vm((2, 128, ROWS), F32), vm((2, 2, 128, ROWS), BF16), vm((NORB, NORB), F32),
          vm((128, NORB), F32), vm((128, NORB), F32), vm((16, 8, NORB), F32),
@@ -509,7 +555,7 @@
          vm((NORB, NORB), F32), vm((2, 128, 2 * ROWS), BF16), vm((2, 3, 32, 128), F32),
          vm((2, 128, 128), F32), vm((2, 128, 128), F32),
          DMA((8,)), DMA((8,)), DMA((16,)), DMA((16,)), DMA((16,)), DMA((16,)), DMA((16,)), DMA((16,)),
-         DMA((8,)), DMA((8,)), DMA, DMA, DMA((16,)), DMA((16,)), DMA((2, 8)), DMA((2, 8)),
+         DMA((8,)), DMA((8,)), DMA, DMA, DMA((16,)), DMA((16,)), DMA((3, 8)), DMA((3, 8)),
          DMA((8,)), DMA((8,)), DMA((16,)), DMA((16,)), DMA((16,)), DMA((16,)),
          DMA((8,)), DMA((8,)), DMA((2, 16)), DMA((2, 16))],
         0, "exchange",

time: 68 us -> 64.5 us (0.949)
  Pallas kernels: 60.9 us -> 57.4 us
    pallas_call x1, Pallas kernels: 60.9 us -> 57.4 us  [call(): pl.pallas_call(kernel, out_shape=[jax.ShapeDtypeStruct(s, d) for s, d in...]
where the time goes in v3:
time: 64.5 us; the launch traced here: 64.2 us
  Pallas kernels  57.4 us (89%)
  local copies, waits for them, and re-layouts  5.95 us (9%)
  between operations  0.71 us (1%)
    pallas_call x1, Pallas kernels, call(): pl.pallas_call(kernel, out_shape=[jax.ShapeDtypeStruct(s, d) for s, d in...  57.4 us
    unnamed x10, local copies, waits for them, and re-layouts  3.02 us

profile of v3, /device:TPU:1, one launch (start us, length us, event | category | flops | bytes accessed | tf_op | source)
XLA Modules:
  0.0 64.2 jit_solution(10575920445801197627)
XLA Ops:
  0.6 1.0 %reshape.25 = f32[2,10,8,3,24]{4,3,2,1,0:T(4,128)S(1)} reshape(bf16[2,5760]{1,0:T(2,128)(2,1)} %param.7) | data formatting | bytes 69120 | tf_op jit(solution)/shard_map/reshape | solution.py:537
  1.6 0.2 copy.25
  1.8 0.2 reshape.32
  2.0 0.0 copy-start.2
  2.0 0.6 %reshape.27.s1_any = f32[8,16,128]{2,1,0:T(8,128)} reshape(f32[8,2,4,256]{3,2,1,0:T(4,128)S(1)} %pad.12.clone) | data formatting | bytes 131072 | tf_op jit(solution)/shard_map/reshape | solution.py:538
  2.6 0.0 copy-done.2
  2.6 0.0 copy-start
  2.6 0.1 broadcast_in_dim.2
  2.7 0.7 %copy-done = bf16[2,5760]{1,0:T(2,128)(2,1)S(1)} copy-done((bf16[2,5760]{1,0:T(2,128)(2,1)S(1)}, bf16[2,5760]{1,0:T(2,128)(2,1)}, u32[]{:S(2)}) %copy-start) | copy-done | bytes 23064
  3.4 0.2 reshape.28
  3.5 0.2 copy.19
  3.8 0.1 select_maximum_fusion
  3.9 0.1 reshape.31
  4.0 0.7 %reshape.30.s2_any = f32[16,8,128]{2,1,0:T(8,128)} reshape(f32[16,2,512]{2,1,0:T(2,128)S(1)} %pad.14.clone) | data formatting | bytes 131072 | tf_op jit(solution)/shard_map/reshape | solution.py:543
  4.7 57.4 %exchange.1 = (f32[2,5760]{1,0:T(2,128)}, f32[2,5760]{1,0:T(2,128)}) custom-call(f32[8,16,128]{2,1,0:T(8,128)} %reshape.27.s1_any, f32[16,8,128]{2,1,0:T(8,128)} %reshape.30.s2_any, bf16[256,512]{1,0:T(8,128)(2,1)} %constant.13.clone.perm_any, bf16[128,1536]{1,0:T(8,128)(2,1)} %constant.14.clone.t_any, bf16[128,128]{1,0:T(8,128)(2,1)} %constant.15.clone.ty_any, ...), custom_call_target="tpu_custom_call" | custom-call | tf_op jit(solution)/shard_map/exchange/pallas_call | solution.py:521
  62.1 0.0 copy-start.1
  62.2 1.4 %copy.29 = f32[2,5760]{1,0:T(2,128)} copy(f32[2,5760]{1,0:T(2,128)} %get-tuple-element.4) | data formatting | bytes 92160
  63.6 0.0 copy-done.1
  63.6 0.6 copy.30
  (2 shorter events, 0.0 us)
Async XLA Ops:
  2.0 0.7 %copy-start.2 = (bf16[2]{0:T(256)(128)(2,1)S(1)}, bf16[2]{0:T(256)(128)(2,1)}, u32[]{:S(2)}) copy-start(bf16[2]{0:T(256)(128)(2,1)} %param.8) | copy-start | bytes 16
  2.6 0.7 %copy-start = (bf16[2,5760]{1,0:T(2,128)(2,1)S(1)}, bf16[2,5760]{1,0:T(2,128)(2,1)}, u32[]{:S(2)}) copy-start(bf16[2,5760]{1,0:T(2,128)(2,1)} %param.7) | copy-start | bytes 69124
  62.1 1.4 %copy-start.1 = (f32[2,5760]{1,0:T(2,128)S(1)}, f32[2,5760]{1,0:T(2,128)}, u32[]{:S(2)}) copy-start(f32[2,5760]{1,0:T(2,128)} %get-tuple-element.5) | copy-start | bytes 138244

commit v4 on v3

--- a/solution.py
+++ b/solution.py
@@ -82,7 +82,7 @@
 def permutations():
     true = np.arange(NORB).reshape(2, 8, 8, 2)
     order_a = true.transpose(0, 2, 1, 3).reshape(-1)
-    order_b = true.transpose(1, 0, 2, 3).reshape(-1)
+    order_b = true.transpose(1, 3, 0, 2).reshape(-1)
     eye = np.eye(NORB, dtype=np.float32)
     return jnp.asarray(np.concatenate([eye[:, order_a], eye[:, order_b]], axis=1), BF16)
 
@@ -143,8 +143,8 @@
 
 
 def main_kernel(
-    s1_any, s2_any, perm_any, t_any, ty_any, right_any, cy_any, ov, oq,
-    s1, s2, perm, t3, ty, right, cy, in_s,
+    st_any, raw_any, oc_any, perm_any, t_any, ty_any, right_any, cy_any, ov, oq,
+    st, raw, oc, s1, s2, cells, turned_cells, perm, t3, ty, right, cy, in_s,
     o1, o2, r1, r2, green, left, y_rows, v_f, v_b, gp, gc, gh, rg, rv, s8, rz,
     gram, vall, tt, dd, rp,
     za_s, za_r, pa_s, pa_r, cg_s, cg_r, cf_s, cf_r, zg_s, zg_r,
@@ -177,7 +177,7 @@
     pl.semaphore_signal(barrier, inc=1, device_id=core_dev, device_id_type=MESH)
 
     held = (
-        (s1_any, s1), (s2_any, s2), (t_any, t3), (ty_any, ty), (cy_any, cy),
+        (raw_any, raw), (oc_any, oc), (st_any, st), (t_any, t3), (ty_any, ty), (cy_any, cy),
         (right_any, right), (perm_any, perm),
     )
     held = [pltpu.make_async_copy(a, b, in_s.at[k]) for k, (a, b) in enumerate(held)]
@@ -186,7 +186,23 @@
     perm_a, perm_b = perm.at[:, :NORB], perm.at[:, NORB:]
     tx, tz, tk = (t3.at[:, k * MODES : (k + 1) * MODES] for k in range(3))
     rh, rl = right.at[:, :512], right.at[:, 512:]
-    for one in held[2:5]:
+    for one in held[:3]:
+        one.wait()
+    cells[...] = jnp.zeros_like(cells)
+    for k in range(45):
+        pair = raw[:, k * 128 : (k + 1) * 128].astype(F32)
+        for o in range(2):
+            cells[64 * o + k : 64 * o + k + 1, :] = pair[o : o + 1]
+    for o in range(2):
+        cells[64 * o + 45 : 64 * o + 46, :] = oc[o : o + 1, :]
+    turned_cells[...] = cells[...].T
+    for k in range(16):
+        s2[k] = turned_cells[pl.ds(k, 8, stride=16), :]
+    for k in range(8):
+        for o in range(2):
+            for part in range(2):
+                s1[k, pl.ds(8 * o + part, 4, stride=2), :] = st[k, o, :4, 128 * part : 128 * part + 128]
+    for one in held[3:6]:
         one.wait()
 
     row = lax.broadcasted_iota(jnp.int32, (ROWS, 128), 0)
@@ -211,8 +227,6 @@
         for hh in range(2):
             green[hh, :, t * 256 : (t + 1) * 256] = g[:, hh * 256 : (hh + 1) * 256]
 
-    for one in held[:2]:
-        one.wait()
     pl.semaphore_wait(barrier, greeted + 1)
 
     def z_send(t):
@@ -231,12 +245,14 @@
     z_line(lambda t: z_send(t).start())
     r1[rows(z * 16, 16)] = s1[z]
     r2[rows(p * 8, 8)] = s2[p]
-    for one in held[5:]:
+    for one in held[6:]:
         one.wait()
     green_part(0)
     swap(16, p, lambda t: p_recv(t).wait_recv())
-    for k in range(3):
-        o2[rows(z * 32, 32), k * 128 : (k + 1) * 128] = r2[pl.ds(k, 32, stride=4), :].astype(BF16)
+    by_row = [r2[pl.ds(k, 16, stride=8), :] for k in range(8)]
+    o2[rows(z * 32, 32), :] = jnp.concatenate(
+        [jnp.concatenate([b[:, 64 * o : 64 * o + 48] for b in by_row], axis=1) for o in range(2)], axis=0
+    ).astype(BF16)
 
     def zg_send(t):
         mine = o2.at[rows(z * 32, 32)]
@@ -532,21 +548,16 @@
 
 
 def on_device(orbitals, occupation):
-    xl, z, y, c, h = me()
-    own = orbitals.astype(F32)
-    s1 = own.reshape(2, 10, 8, 3, NZ).transpose(2, 0, 3, 1, 4).reshape(8, 2, 3, 240)
-    s1 = jnp.pad(s1, ((0, 0), (0, 0), (0, 1), (0, 16))).reshape(8, 16, 128)
-    s2 = own.reshape(2, 45, 8, 16).transpose(3, 0, 2, 1)
-    occ = jnp.broadcast_to(occupation.astype(F32)[None, :, None, None], (16, 2, 8, 1))
-    s2 = jnp.concatenate([s2, occ], axis=3)
-    s2 = jnp.pad(s2, ((0, 0), (0, 0), (0, 0), (0, 2))).reshape(16, 2, ROWS)
-    s2 = jnp.pad(s2, ((0, 0), (0, 0), (0, 128))).reshape(16, 8, 128)
+    st = orbitals.astype(F32).reshape(2, 10, 8, 3, NZ).transpose(2, 0, 3, 1, 4).reshape(8, 2, 3, 240)
+    st = jnp.pad(st, ((0, 0), (0, 0), (0, 5), (0, 16)))
+    occ = jnp.broadcast_to(occupation.astype(F32)[:, None], (2, 128))
     vm = pltpu.VMEM
     return tuple(call(
-        main_kernel, (s1, s2, permutations(), *tables()),
+        main_kernel, (st, orbitals, occ, permutations(), *tables()),
         (((2, HALF), F32), ((2, HALF), F32)),
-        [vm((8, 16, 128), F32), vm((16, 8, 128), F32), vm((NORB, 512), BF16), vm((128, 3 * MODES), BF16),
-         vm((128, 128), BF16), vm((MODES, 1024), BF16), vm((32, 128), F32), DMA((7,)),
+        [vm((8, 2, 8, 256), F32), vm((2, HALF), BF16), vm((2, 128), F32),
+         vm((8, 16, 128), F32), vm((16, 8, 128), F32), vm((128, 128), F32), vm((128, 128), F32), vm((NORB, 512), BF16), vm((128, 3 * MODES), BF16),
+         vm((128, 128), BF16), vm((MODES, 1024), BF16), vm((32, 128), F32), DMA((8,)),
          vm((2, NORB, 768), BF16), vm((NORB, ROWS), BF16), vm((128, 128), F32), vm((128, 128), F32),
          vm((2, ROWS, 768), F32), vm((ROWS, MODES), F32), vm((ROWS, 128), F32),
          vm((2, 128, ROWS), F32), vm((2, 2, 128, ROWS), BF16), vm((NORB, NORB), F32),

time: 64.5 us -> 62.9 us (0.975)
  local copies, waits for them, and re-layouts: 5.95 us -> 3.86 us
    reshape x5 -> x3, local copies, waits for them, and re-layouts: 2.61 us -> 1.17 us  [on_device(): orbitals.astype(F32).reshape(2, 10, 8, 3, NZ).transpose(2, 0, 3, 1, 4)]
    unnamed x10 -> x6, local copies, waits for them, and re-layouts: 3.02 us -> 2.05 us
    pad x0 -> x1, other arithmetic: none -> 0.66 us  [on_device(): st = jnp.pad(st, ((0, 0), (0, 0), (0, 5), (0, 16)))]
where the time goes in v4:
time: 62.9 us; the launch traced here: 62.6 us
  Pallas kernels  57.4 us (91%)
  local copies, waits for them, and re-layouts  3.86 us (6%)
  between operations  0.67 us (1%)
  other arithmetic  0.66 us (1%)
    pallas_call x1, Pallas kernels, call(): pl.pallas_call(kernel, out_shape=[jax.ShapeDtypeStruct(s, d) for s, d in...  57.4 us
    unnamed x6, local copies, waits for them, and re-layouts  2.05 us

profile of v4, /device:TPU:1, one launch (start us, length us, event | category | flops | bytes accessed | tf_op | source)
XLA Modules:
  0.0 62.6 jit_solution(2746819631812545667)
XLA Ops:
  0.6 0.9 %reshape.13 = bf16[2,10,8,3,24]{4,3,2,1,0:T(4,128)(2,1)S(1)} reshape(bf16[2,5760]{1,0:T(2,128)(2,1)} %raw_any.1) | data formatting | bytes 46080 | tf_op jit(solution)/shard_map/reshape | solution.py:551
  1.6 0.1 copy.12
  1.6 0.2 reshape.15
  1.8 0.0 copy-start.1
  1.8 0.7 %pad_convert_fusion.st_any = f32[8,2,8,256]{3,2,1,0:T(8,128)} fusion(bf16[8,2,3,240]{3,2,1,0:T(4,128)(2,1)S(1)} %reshape.15), kind=kLoop, calls=%fused_computation | loop fusion | flops 32768 | bytes 154112 | tf_op jit(solution)/shard_map/jit(_pad)/pad | solution.py:552
  2.5 0.0 copy-done.1
  2.5 0.6 %broadcast_in_dim.2.oc_any = f32[2,128]{1,0:T(2,128)} broadcast(bf16[2]{0:T(256)(128)(2,1)S(1)} %copy-done.1), dimensions={0} | broadcast | bytes 1028 | tf_op jit(solution)/shard_map/broadcast_in_dim | solution.py:553
  3.1 57.4 %exchange.1 = (f32[2,5760]{1,0:T(2,128)}, f32[2,5760]{1,0:T(2,128)}) custom-call(f32[8,2,8,256]{3,2,1,0:T(8,128)} %pad_convert_fusion.st_any, bf16[2,5760]{1,0:T(2,128)(2,1)} %raw_any.1, f32[2,128]{1,0:T(2,128)} %broadcast_in_dim.2.oc_any, bf16[256,512]{1,0:T(8,128)(2,1)} %constant.14.clone.perm_any, bf16[128,1536]{1,0:T(8,128)(2,1)} %constant.15.clone.t_any, ...), custom_call_target="tpu_custom_call" | custom-call | tf_op jit(solution)/shard_map/exchange/pallas_call | solution.py:537
  60.6 0.0 copy-start
  60.6 1.4 %copy.16 = f32[2,5760]{1,0:T(2,128)} copy(f32[2,5760]{1,0:T(2,128)} %get-tuple-element.4) | data formatting | bytes 92160
  62.0 0.0 copy-done
  62.0 0.6 copy.17
Async XLA Ops:
  1.8 0.7 %copy-start.1 = (bf16[2]{0:T(256)(128)(2,1)S(1)}, bf16[2]{0:T(256)(128)(2,1)}, u32[]{:S(2)}) copy-start(bf16[2]{0:T(256)(128)(2,1)} %param.8) | copy-start | bytes 16
  60.6 1.4 %copy-start = (f32[2,5760]{1,0:T(2,128)S(1)}, f32[2,5760]{1,0:T(2,128)}, u32[]{:S(2)}) copy-start(f32[2,5760]{1,0:T(2,128)} %get-tuple-element.5) | copy-start | bytes 138244

commit v5 on v4

--- a/solution.py
+++ b/solution.py
@@ -143,8 +143,8 @@
 
 
 def main_kernel(
-    st_any, raw_any, oc_any, perm_any, t_any, ty_any, right_any, cy_any, ov, oq,
-    st, raw, oc, s1, s2, cells, turned_cells, perm, t3, ty, right, cy, in_s,
+    st_any, raw_any, perm_any, t_any, ty_any, right_any, cy_any, results,
+    st, raw, s1, s2, cells, turned_cells, perm, t3, ty, right, cy, in_s,
     o1, o2, r1, r2, green, left, y_rows, v_f, v_b, gp, gc, gh, rg, rv, s8, rz,
     gram, vall, tt, dd, rp,
     za_s, za_r, pa_s, pa_r, cg_s, cg_r, cf_s, cf_r, zg_s, zg_r,
@@ -177,7 +177,7 @@
     pl.semaphore_signal(barrier, inc=1, device_id=core_dev, device_id_type=MESH)
 
     held = (
-        (raw_any, raw), (oc_any, oc), (st_any, st), (t_any, t3), (ty_any, ty), (cy_any, cy),
+        (raw_any, raw), (st_any, st), (t_any, t3), (ty_any, ty), (cy_any, cy),
         (right_any, right), (perm_any, perm),
     )
     held = [pltpu.make_async_copy(a, b, in_s.at[k]) for k, (a, b) in enumerate(held)]
@@ -186,7 +186,7 @@
     perm_a, perm_b = perm.at[:, :NORB], perm.at[:, NORB:]
     tx, tz, tk = (t3.at[:, k * MODES : (k + 1) * MODES] for k in range(3))
     rh, rl = right.at[:, :512], right.at[:, 512:]
-    for one in held[:3]:
+    for one in held[:2]:
         one.wait()
     cells[...] = jnp.zeros_like(cells)
     for k in range(45):
@@ -194,7 +194,7 @@
         for o in range(2):
             cells[64 * o + k : 64 * o + k + 1, :] = pair[o : o + 1]
     for o in range(2):
-        cells[64 * o + 45 : 64 * o + 46, :] = oc[o : o + 1, :]
+        cells[64 * o + 45 : 64 * o + 46, :] = st[0, o, 3:4, :128]
     turned_cells[...] = cells[...].T
     for k in range(16):
         s2[k] = turned_cells[pl.ds(k, 8, stride=16), :]
@@ -202,7 +202,7 @@
         for o in range(2):
             for part in range(2):
                 s1[k, pl.ds(8 * o + part, 4, stride=2), :] = st[k, o, :4, 128 * part : 128 * part + 128]
-    for one in held[3:6]:
+    for one in held[2:5]:
         one.wait()
 
     row = lax.broadcasted_iota(jnp.int32, (ROWS, 128), 0)
@@ -245,7 +245,7 @@
     z_line(lambda t: z_send(t).start())
     r1[rows(z * 16, 16)] = s1[z]
     r2[rows(p * 8, 8)] = s2[p]
-    for one in held[6:]:
+    for one in held[5:]:
         one.wait()
     green_part(0)
     swap(16, p, lambda t: p_recv(t).wait_recv())
@@ -382,7 +382,7 @@
     for part in range(3):
         swap(8, z, lambda t, part=part: v_recv(part, t).wait_recv())
     others = jnp.sum(rv[0].astype(F32) + rv[1].astype(F32), axis=0)
-    mine = -(v_f[:, rows(z * 16, 16), :] + others)
+    mine = v_f[:, rows(z * 16, 16), :] + others
     m_high, m_low = split2(mine)
     own = vall.at[:, rows(z * 16, 16), :]
     own[:, :, :ROWS] = m_high
@@ -425,12 +425,12 @@
         half(lambda t: d_send(n, t).start())
         rp[n, rows(p * 8, 8)] = dd[n, rows(p * 8, 8)]
 
-    def land(n, out):
+    def land(n):
         swap(16, p, lambda t: d_recv(n, t).wait_recv())
         table = jnp.concatenate([rp[n, pl.ds(k, 16, stride=8), :] for k in range(8)], axis=0)
         turned = table.T
         for k in range(45):
-            out[:, k * 128 : (k + 1) * 128] = jnp.concatenate(
+            results[n, :, k * 128 : (k + 1) * 128] = jnp.concatenate(
                 [turned[k : k + 1], turned[64 + k : 65 + k]], axis=0
             )
 
@@ -447,7 +447,7 @@
     swap(8, z, lambda t: vg_recv(t).wait_recv())
     out = dot(l_both, vall[...].reshape(NORB, 2 * ROWS))
     deal(1, out[:32, :ROWS] + out[32:, :ROWS] + out[:32, ROWS:])
-    land(0, ov)
+    land(0)
     for group, i, sends in (
         (8, z, (z_send, zg_send, *(functools.partial(v_send, k) for k in range(3)), gz_send, vg_send)),
         (16, p, (p_send, functools.partial(d_send, 0))),
@@ -456,7 +456,7 @@
         for send in sends:
             swap(group, i, lambda t, send=send: send(t).wait_send())
     each(16, lambda t: f_send(t).wait_send())
-    land(1, oq)
+    land(1)
     swap(16, p, lambda t: d_send(1, t).wait_send())
 
 
@@ -550,12 +550,13 @@
 def on_device(orbitals, occupation):
     st = orbitals.astype(F32).reshape(2, 10, 8, 3, NZ).transpose(2, 0, 3, 1, 4).reshape(8, 2, 3, 240)
     st = jnp.pad(st, ((0, 0), (0, 0), (0, 5), (0, 16)))
-    occ = jnp.broadcast_to(occupation.astype(F32)[:, None], (2, 128))
+    spare = lax.broadcasted_iota(jnp.int32, st.shape, 2) == 3
+    st = jnp.where(spare, occupation.astype(F32)[None, :, None, None], st)
     vm = pltpu.VMEM
-    return tuple(call(
-        main_kernel, (st, orbitals, occ, permutations(), *tables()),
-        (((2, HALF), F32), ((2, HALF), F32)),
-        [vm((8, 2, 8, 256), F32), vm((2, HALF), BF16), vm((2, 128), F32),
+    both = call(
+        main_kernel, (st, orbitals, permutations(), *tables()),
+        (((2, 2, HALF), F32),),
+        [vm((8, 2, 8, 256), F32), vm((2, HALF), BF16),
          vm((8, 16, 128), F32), vm((16, 8, 128), F32), vm((128, 128), F32), vm((128, 128), F32), vm((NORB, 512), BF16), vm((128, 3 * MODES), BF16),
          vm((128, 128), BF16), vm((MODES, 1024), BF16), vm((32, 128), F32), DMA((8,)),
          vm((2, NORB, 768), BF16), vm((NORB, ROWS), BF16), vm((128, 128), F32), vm((128, 128), F32),
@@ -570,7 +571,8 @@
          DMA((8,)), DMA((8,)), DMA((16,)), DMA((16,)), DMA((16,)), DMA((16,)),
          DMA((8,)), DMA((8,)), DMA((2, 16)), DMA((2, 16))],
         0, "exchange",
-    ))
+    )[0]
+    return -both[0], -both[1]
 
 
 def solution(mesh):

time: 62.9 us -> 62.2 us (0.989)
  local copies, waits for them, and re-layouts: 3.86 us -> 1.65 us
  other arithmetic: 0.66 us -> 2.21 us
    unnamed x6 -> x2, local copies, waits for them, and re-layouts: 2.05 us -> 0.48 us
    neg x0 -> x1, other arithmetic: none -> 1.49 us  [on_device(): return (-both[0], -both[1])]
    select_n x0 -> x1, other arithmetic: none -> 0.72 us  [on_device(): st = jnp.where(spare, occupation.astype(F32)[None, :, None, None], st)]
    pad x1 -> x0, other arithmetic: 0.66 us -> none  [on_device(): st = jnp.pad(st, ((0, 0), (0, 0), (0, 5), (0, 16)))]
    broadcast_in_dim x1 -> x0, local copies, waits for them, and re-layouts: 0.63 us -> none  [on_device(): occ = jnp.broadcast_to(occupation.astype(F32)[:, None], (2, 128))]
where the time goes in v5:
time: 62.2 us; the launch traced here: 62 us
  Pallas kernels  57.5 us (92%)
  other arithmetic  2.21 us (4%)
  local copies, waits for them, and re-layouts  1.65 us (3%)
  between operations  0.66 us (1%)
    pallas_call x1, Pallas kernels, call(): pl.pallas_call(kernel, out_shape=[jax.ShapeDtypeStruct(s, d) for s, d in...  57.5 us
    neg x1, other arithmetic, on_device(): return (-both[0], -both[1])  1.49 us

profile of v5, /device:TPU:1, one launch (start us, length us, event | category | flops | bytes accessed | tf_op | source)
XLA Modules:
  0.0 62.0 jit_solution(12120337408677721120)
XLA Ops:
  0.6 0.9 %reshape.15 = bf16[2,10,8,3,24]{4,3,2,1,0:T(4,128)(2,1)S(1)} reshape(bf16[2,5760]{1,0:T(2,128)(2,1)} %raw_any.1) | data formatting | bytes 46080 | tf_op jit(solution)/shard_map/reshape | solution.py:551
  1.6 0.1 copy.12
  1.6 0.0 copy-start
  1.7 0.2 reshape.17
  1.8 0.5 copy-done
  2.3 0.7 %convert_select_fusion.st_any = f32[8,2,8,256]{3,2,1,0:T(8,128)} fusion(bf16[8,2,3,240]{3,2,1,0:T(4,128)(2,1)S(1)} %reshape.17, f32[2]{0:T(128)S(1)} %convert_element_type.6, pred[8]{0:T(512)(128)(4,1)S(1)} %iota_compare_fusion), kind=kLoop, calls=%fused_computation | loop fusion | flops 65536 | bytes 154128 | tf_op jit(solution)/shard_map/jit(_where)/select_n | solution.py:554
  3.0 57.5 %exchange.1 = f32[2,2,5760]{2,1,0:T(2,128)} custom-call(f32[8,2,8,256]{3,2,1,0:T(8,128)} %convert_select_fusion.st_any, bf16[2,5760]{1,0:T(2,128)(2,1)} %raw_any.1, bf16[256,512]{1,0:T(8,128)(2,1)} %constant.16.clone.perm_any, bf16[128,1536]{1,0:T(8,128)(2,1)} %constant.17.clone.t_any, bf16[128,128]{1,0:T(8,128)(2,1)} %constant.18.clone.ty_any, ...), custom_call_target="tpu_custom_call" | custom-call | tf_op jit(solution)/shard_map/exchange/pallas_call | solution.py:537
  60.5 1.5 %negate_bitcast_fusion = (f32[2,5760]{1,0:T(2,128)}, f32[2,5760]{1,0:T(2,128)}) fusion(f32[2,2,5760]{2,1,0:T(2,128)} %exchange.1), kind=kLoop, calls=%fused_computation.1 | loop fusion | flops 23040 | bytes 184320 | tf_op jit(solution)/shard_map/neg | solution.py:575
  (2 shorter events, 0.0 us)
Async XLA Ops:
  1.6 0.7 %copy-start = (bf16[2]{0:T(256)(128)(2,1)S(1)}, bf16[2]{0:T(256)(128)(2,1)}, u32[]{:S(2)}) copy-start(bf16[2]{0:T(256)(128)(2,1)} %param.8) | copy-start | bytes 16

commit v6 on v5

--- a/solution.py
+++ b/solution.py
@@ -143,8 +143,8 @@
 
 
 def main_kernel(
-    st_any, raw_any, perm_any, t_any, ty_any, right_any, cy_any, results,
-    st, raw, s1, s2, cells, turned_cells, perm, t3, ty, right, cy, in_s,
+    st_any, raw_any, oc_any, perm_any, t_any, ty_any, right_any, cy_any, results,
+    st, raw, oc, s1, by_y, s2, cells, turned_cells, perm, t3, ty, right, cy, in_s,
     o1, o2, r1, r2, green, left, y_rows, v_f, v_b, gp, gc, gh, rg, rv, s8, rz,
     gram, vall, tt, dd, rp,
     za_s, za_r, pa_s, pa_r, cg_s, cg_r, cf_s, cf_r, zg_s, zg_r,
@@ -177,7 +177,7 @@
     pl.semaphore_signal(barrier, inc=1, device_id=core_dev, device_id_type=MESH)
 
     held = (
-        (raw_any, raw), (st_any, st), (t_any, t3), (ty_any, ty), (cy_any, cy),
+        (raw_any, raw), (oc_any, oc), (st_any, st), (t_any, t3), (ty_any, ty), (cy_any, cy),
         (right_any, right), (perm_any, perm),
     )
     held = [pltpu.make_async_copy(a, b, in_s.at[k]) for k, (a, b) in enumerate(held)]
@@ -186,7 +186,7 @@
     perm_a, perm_b = perm.at[:, :NORB], perm.at[:, NORB:]
     tx, tz, tk = (t3.at[:, k * MODES : (k + 1) * MODES] for k in range(3))
     rh, rl = right.at[:, :512], right.at[:, 512:]
-    for one in held[:2]:
+    for one in held[:3]:
         one.wait()
     cells[...] = jnp.zeros_like(cells)
     for k in range(45):
@@ -194,15 +194,20 @@
         for o in range(2):
             cells[64 * o + k : 64 * o + k + 1, :] = pair[o : o + 1]
     for o in range(2):
-        cells[64 * o + 45 : 64 * o + 46, :] = st[0, o, 3:4, :128]
+        cells[64 * o + 45 : 64 * o + 46, :] = jnp.broadcast_to(oc[...].astype(F32)[None, o : o + 1], (1, 128))
     turned_cells[...] = cells[...].T
     for k in range(16):
         s2[k] = turned_cells[pl.ds(k, 8, stride=16), :]
-    for k in range(8):
-        for o in range(2):
-            for part in range(2):
-                s1[k, pl.ds(8 * o + part, 4, stride=2), :] = st[k, o, :4, 128 * part : 128 * part + 128]
-    for one in held[2:5]:
+    s1[...] = jnp.zeros_like(s1)
+    for o in range(2):
+        wide_rows = jnp.concatenate(
+            [st[o, k].astype(F32) for k in range(10)] + [jnp.zeros((NY, 16), F32)], axis=1
+        )
+        for part in range(2):
+            by_y[o, part] = wide_rows[:, 128 * part : 128 * part + 128]
+            for t in range(3):
+                s1[pl.ds(8 * o + 2 * t + part, 8, stride=16), :] = by_y[o, part, pl.ds(t, 8, stride=3), :]
+    for one in held[3:6]:
         one.wait()
 
     row = lax.broadcasted_iota(jnp.int32, (ROWS, 128), 0)
@@ -230,10 +235,10 @@
     pl.semaphore_wait(barrier, greeted + 1)
 
     def z_send(t):
-        return copy(s1.at[t], r1.at[rows(z * 16, 16)], za_s.at[t], za_r.at[z], z_dev(t))
+        return copy(s1.at[rows(t * 16, 16)], r1.at[rows(z * 16, 16)], za_s.at[t], za_r.at[z], z_dev(t))
 
     def z_recv(t):
-        return copy(s1.at[t], r1.at[rows(t * 16, 16)], za_s.at[t], za_r.at[t], z_dev(t))
+        return copy(s1.at[rows(t * 16, 16)], r1.at[rows(t * 16, 16)], za_s.at[t], za_r.at[t], z_dev(t))
 
     def p_send(t):
         return copy(s2.at[t], r2.at[rows(p * 8, 8)], pa_s.at[t], pa_r.at[p], half_dev(t))
@@ -243,9 +248,9 @@
 
     half(lambda t: p_send(t).start())
     z_line(lambda t: z_send(t).start())
-    r1[rows(z * 16, 16)] = s1[z]
+    r1[rows(z * 16, 16)] = s1[rows(z * 16, 16)]
     r2[rows(p * 8, 8)] = s2[p]
-    for one in held[5:]:
+    for one in held[6:]:
         one.wait()
     green_part(0)
     swap(16, p, lambda t: p_recv(t).wait_recv())
@@ -548,16 +553,13 @@
 
 
 def on_device(orbitals, occupation):
-    st = orbitals.astype(F32).reshape(2, 10, 8, 3, NZ).transpose(2, 0, 3, 1, 4).reshape(8, 2, 3, 240)
-    st = jnp.pad(st, ((0, 0), (0, 0), (0, 5), (0, 16)))
-    spare = lax.broadcasted_iota(jnp.int32, st.shape, 2) == 3
-    st = jnp.where(spare, occupation.astype(F32)[None, :, None, None], st)
+    planes = orbitals.reshape(2, 10, NY, NZ)
     vm = pltpu.VMEM
     both = call(
-        main_kernel, (st, orbitals, permutations(), *tables()),
+        main_kernel, (planes, orbitals, occupation, permutations(), *tables()),
         (((2, 2, HALF), F32),),
-        [vm((8, 2, 8, 256), F32), vm((2, HALF), BF16),
-         vm((8, 16, 128), F32), vm((16, 8, 128), F32), vm((128, 128), F32), vm((128, 128), F32), vm((NORB, 512), BF16), vm((128, 3 * MODES), BF16),
+        [vm((2, 10, NY, NZ), BF16), vm((2, HALF), BF16), vm((2,), BF16),
+         vm((128, 128), F32), vm((2, 2, NY, 128), F32), vm((16, 8, 128), F32), vm((128, 128), F32), vm((128, 128), F32), vm((NORB, 512), BF16), vm((128, 3 * MODES), BF16),
          vm((128, 128), BF16), vm((MODES, 1024), BF16), vm((32, 128), F32), DMA((8,)),
          vm((2, NORB, 768), BF16), vm((NORB, ROWS), BF16), vm((128, 128), F32), vm((128, 128), F32),
          vm((2, ROWS, 768), F32), vm((ROWS, MODES), F32), vm((ROWS, 128), F32),

time: 62.2 us -> 61.4 us (0.987)
  other arithmetic: 2.21 us -> 1.49 us
    select_n x1 -> x0, other arithmetic: 0.72 us -> none  [on_device(): st = jnp.where(spare, occupation.astype(F32)[None, :, None, None], st)]
    reshape x3 -> x1, local copies, waits for them, and re-layouts: 1.17 us -> 1.58 us  [on_device(): planes = orbitals.reshape(2, 10, NY, NZ)]
where the time goes in v6:
time: 61.4 us; the launch traced here: 61.1 us
  Pallas kernels  57.4 us (93%)
  local copies, waits for them, and re-layouts  1.58 us (3%)
  other arithmetic  1.49 us (2%)
  between operations  0.64 us (1%)
    pallas_call x1, Pallas kernels, call(): pl.pallas_call(kernel, out_shape=[jax.ShapeDtypeStruct(s, d) for s, d in...  57.4 us
    reshape x1, local copies, waits for them, and re-layouts, on_device(): planes = orbitals.reshape(2, 10, NY, NZ)  1.58 us
    neg x1, other arithmetic, on_device(): return (-both[0], -both[1])  1.49 us

profile of v6, /device:TPU:1, one launch (start us, length us, event | category | flops | bytes accessed | tf_op | source)
XLA Modules:
  0.0 61.1 jit_solution(18044255495646316581)
XLA Ops:
  0.6 1.6 %reshape.9.st_any = bf16[2,10,24,24]{3,2,1,0:T(8,128)(2,1)} reshape(bf16[2,5760]{1,0:T(2,128)(2,1)} %raw_any.1) | data formatting | bytes 46080 | tf_op jit(solution)/shard_map/reshape | solution.py:556
  2.2 57.4 %exchange.1 = f32[2,2,5760]{2,1,0:T(2,128)} custom-call(bf16[2,10,24,24]{3,2,1,0:T(8,128)(2,1)} %reshape.9.st_any, bf16[2,5760]{1,0:T(2,128)(2,1)} %raw_any.1, bf16[2]{0:T(256)(128)(2,1)} %oc_any.1, bf16[256,512]{1,0:T(8,128)(2,1)} %constant.10.clone.perm_any, bf16[128,1536]{1,0:T(8,128)(2,1)} %constant.11.clone.t_any, ...), custom_call_target="tpu_custom_call" | custom-call | tf_op jit(solution)/shard_map/exchange/pallas_call | solution.py:542
  59.6 1.5 %negate_bitcast_fusion = (f32[2,5760]{1,0:T(2,128)}, f32[2,5760]{1,0:T(2,128)}) fusion(f32[2,2,5760]{2,1,0:T(2,128)} %exchange.1), kind=kLoop, calls=%fused_computation | loop fusion | flops 23040 | bytes 184320 | tf_op jit(solution)/shard_map/neg | solution.py:577

commit v7 on v6

--- a/solution.py
+++ b/solution.py
@@ -207,8 +207,6 @@
             by_y[o, part] = wide_rows[:, 128 * part : 128 * part + 128]
             for t in range(3):
                 s1[pl.ds(8 * o + 2 * t + part, 8, stride=16), :] = by_y[o, part, pl.ds(t, 8, stride=3), :]
-    for one in held[3:6]:
-        one.wait()
 
     row = lax.broadcasted_iota(jnp.int32, (ROWS, 128), 0)
     lane = lax.broadcasted_iota(jnp.int32, (ROWS, 128), 1)
@@ -220,8 +218,6 @@
     y_cell = shifted(yz, 2731, 16)
     z_cell = yz - y_cell * NZ
     hot = lambda a: jnp.where(a == lane, 1.0, 0.0).astype(BF16)
-    left[...] = dot(hot(jnp.where(s < 45, x, 127)), tx[...]) * dot(hot(z_cell), tz[...])
-    y_rows[...] = dot(hot(y_cell), ty[...])
     middle = (lane >= 32) & (lane < 64)
 
     def green_part(t):
@@ -250,8 +246,10 @@
     z_line(lambda t: z_send(t).start())
     r1[rows(z * 16, 16)] = s1[rows(z * 16, 16)]
     r2[rows(p * 8, 8)] = s2[p]
-    for one in held[6:]:
+    for one in held[3:]:
         one.wait()
+    left[...] = dot(hot(jnp.where(s < 45, x, 127)), tx[...]) * dot(hot(z_cell), tz[...])
+    y_rows[...] = dot(hot(y_cell), ty[...])
     green_part(0)
     swap(16, p, lambda t: p_recv(t).wait_recv())
     by_row = [r2[pl.ds(k, 16, stride=8), :] for k in range(8)]

time: 61.4 us -> 61.3 us (level)
  no operation moved by 1% of the time
where the time goes in v7:
time: 61.3 us; the launch traced here: 61.1 us
  Pallas kernels  57.4 us (94%)
  local copies, waits for them, and re-layouts  1.58 us (3%)
  other arithmetic  1.49 us (2%)
  between operations  0.64 us (1%)
    pallas_call x1, Pallas kernels, call(): pl.pallas_call(kernel, out_shape=[jax.ShapeDtypeStruct(s, d) for s, d in...  57.4 us
    reshape x1, local copies, waits for them, and re-layouts, on_device(): planes = orbitals.reshape(2, 10, NY, NZ)  1.58 us
    neg x1, other arithmetic, on_device(): return (-both[0], -both[1])  1.49 us

profile of v7, /device:TPU:1, one launch (start us, length us, event | category | flops | bytes accessed | tf_op | source)
XLA Modules:
  0.0 61.1 jit_solution(16728772222624169743)
XLA Ops:
  0.6 1.6 %reshape.9.st_any = bf16[2,10,24,24]{3,2,1,0:T(8,128)(2,1)} reshape(bf16[2,5760]{1,0:T(2,128)(2,1)} %raw_any.1) | data formatting | bytes 46080 | tf_op jit(solution)/shard_map/reshape | solution.py:554
  2.2 57.4 %exchange.1 = f32[2,2,5760]{2,1,0:T(2,128)} custom-call(bf16[2,10,24,24]{3,2,1,0:T(8,128)(2,1)} %reshape.9.st_any, bf16[2,5760]{1,0:T(2,128)(2,1)} %raw_any.1, bf16[2]{0:T(256)(128)(2,1)} %oc_any.1, bf16[256,512]{1,0:T(8,128)(2,1)} %constant.10.clone.perm_any, bf16[128,1536]{1,0:T(8,128)(2,1)} %constant.11.clone.t_any, ...), custom_call_target="tpu_custom_call" | custom-call | tf_op jit(solution)/shard_map/exchange/pallas_call | solution.py:540
  59.6 1.5 %negate_bitcast_fusion = (f32[2,5760]{1,0:T(2,128)}, f32[2,5760]{1,0:T(2,128)}) fusion(f32[2,2,5760]{2,1,0:T(2,128)} %exchange.1), kind=kLoop, calls=%fused_computation | loop fusion | flops 23040 | bytes 184320 | tf_op jit(solution)/shard_map/neg | solution.py:575

commit v8 on v7

--- a/solution.py
+++ b/solution.py
@@ -404,7 +404,6 @@
         g_recv(t).wait_recv()
         gf_send(t).start()
 
-    chips(g_pass_on)
 
     def d_send(n, t):
         return copy(dd.at[n, rows(t * 8, 8)], rp.at[n, rows(p * 8, 8)], d_s.at[n, t], d_r.at[n, p], half_dev(t))
@@ -438,6 +437,7 @@
             )
 
     deal(0, mine.reshape(32, ROWS))
+    chips(g_pass_on)
     each(16, lambda t: gf_recv(t).wait_recv())
     half_send().wait_send()
     swap(16, q, lambda t: g_send(t).wait_send())

time: 61.3 us -> 61.4 us (level)
  no operation moved by 1% of the time
where the time goes in v8:
time: 61.4 us; the launch traced here: 61.1 us
  Pallas kernels  57.4 us (93%)
  local copies, waits for them, and re-layouts  1.58 us (3%)
  other arithmetic  1.49 us (2%)
  between operations  0.64 us (1%)
    pallas_call x1, Pallas kernels, call(): pl.pallas_call(kernel, out_shape=[jax.ShapeDtypeStruct(s, d) for s, d in...  57.4 us
    reshape x1, local copies, waits for them, and re-layouts, on_device(): planes = orbitals.reshape(2, 10, NY, NZ)  1.58 us
    neg x1, other arithmetic, on_device(): return (-both[0], -both[1])  1.49 us

profile of v8, /device:TPU:1, one launch (start us, length us, event | category | flops | bytes accessed | tf_op | source)
XLA Modules:
  0.0 61.1 jit_solution(5695108253184784872)
XLA Ops:
  0.6 1.6 %reshape.9.st_any = bf16[2,10,24,24]{3,2,1,0:T(8,128)(2,1)} reshape(bf16[2,5760]{1,0:T(2,128)(2,1)} %raw_any.1) | data formatting | bytes 46080 | tf_op jit(solution)/shard_map/reshape | solution.py:554
  2.2 57.4 %exchange.1 = f32[2,2,5760]{2,1,0:T(2,128)} custom-call(bf16[2,10,24,24]{3,2,1,0:T(8,128)(2,1)} %reshape.9.st_any, bf16[2,5760]{1,0:T(2,128)(2,1)} %raw_any.1, bf16[2]{0:T(256)(128)(2,1)} %oc_any.1, bf16[256,512]{1,0:T(8,128)(2,1)} %constant.10.clone.perm_any, bf16[128,1536]{1,0:T(8,128)(2,1)} %constant.11.clone.t_any, ...), custom_call_target="tpu_custom_call" | custom-call | tf_op jit(solution)/shard_map/exchange/pallas_call | solution.py:540
  59.6 1.5 %negate_bitcast_fusion = (f32[2,5760]{1,0:T(2,128)}, f32[2,5760]{1,0:T(2,128)}) fusion(f32[2,2,5760]{2,1,0:T(2,128)} %exchange.1), kind=kLoop, calls=%fused_computation | loop fusion | flops 23040 | bytes 184320 | tf_op jit(solution)/shard_map/neg | solution.py:575
